TPU v7x, 128 devices: a whole 4x4x4 slice. The times are simulated.
128 devices in a mesh: chan: 4 (over x), rows: 32 (over z, y, core).
Axes of the slice: x: 4, y: 4, z: 4, core: 2. Of those that a mesh axis runs over, the one named last changes fastest.
Arguments:
- residual: float32 [4, 1024, 16384], P('chan', 'rows'), may hold values from -6 to 6
- psf: float32 [4, 2048, 2048], P('chan', 'rows'), may hold values from -2 to 2
- positions: int32 [32, 2], replicated, may hold values from 0 to 15360, as said below
Outputs:
- residual_out: float32 [4, 1024, 16384], P('chan', 'rows')
- normalized: float32 [1024, 16384], P('rows', 'chan')
Inputs may be any that keep to these rules, and one draw needn't show every extreme that they name: positions[k, 0] is a row of the image, 0 to 1023; positions[k, 1] is a column from 1024 to 15360.
All inputs are finite; a program needn't handle non-finite values.
Results may differ from a plain program's by a relative error of at most 0.0001.
Values sent between devices are 32-bit elements; how exact they have to be, the bound alone decides.
No kernel may reach another device: no remote copies, remote signals or barrier semaphores. Data moves between devices by JAX's collectives and lax.ppermute only.
A program may use at most 128 MiB of HBM per device.

v0:
```python
import functools

import jax
import jax.numpy as jnp
from jax import lax
from jax.experimental import pallas as pl
from jax.experimental.pallas import tpu as pltpu
from jax.sharding import Mesh
from jax.sharding import PartitionSpec as P


STEPS = 32
ROWS = ("rows_0", "rows_1", "rows_2")
CHAN_ROWS = ("chan", "rows_0", "rows_1", "rows_2")
LANES = 128
SUBLANES = 8
DEVICES = 128
NCHAN = 4
SLAB = 32
SHARD = 64
PATCH = 2048
HALF = PATCH // 2
NCOL = 16384
TALL = SLAB + SUBLANES
FOLD = LANES // STEPS
QUARTER = NCOL // NCHAN
SLOTS = 10
EDGE = 32
PART_VMEM = 40 << 20
JOIN_VMEM = 12 << 20
EARLY = (("own", 0), ("own", 1), ("own", 2), ("own", 3), ("near", 0), ("near", 1), ("near", 3))
LATE = (("near_outer", 2), ("near_inner", 2), ("far", 0), ("far", 1), ("far", 2), ("far", 3))
PIECES = (
    (0, 0, 32),
    (1, 0, 16),
    (1, 16, 16),
    (2, 0, 16),
    (2, 16, 16),
    (3, 0, 16),
    (3, 16, 16),
)


def place_of_rows():
    return lax.axis_index("rows_0") * 8 + lax.axis_index("rows_1") * 2 + lax.axis_index("rows_2")


def floor_to(x, size):
    return pl.multiple_of(x - (x & (size - 1)), size)


def table_kernel(pos_ref, psf_ref, res_ref, out_ref, tiles, wide, acc, sems):
    row_id = place_of_rows()
    first = row_id * SLAB
    lane = lax.broadcasted_iota(jnp.int32, (SUBLANES, LANES), 1)
    cell = lax.broadcasted_iota(jnp.int32, (SUBLANES, LANES), 0) * LANES + lane

    def tile_copy(k):
        local = (pos_ref[0, k] - first) & (SLAB - 1)
        src = res_ref.at[pl.ds(floor_to(local, SUBLANES), SUBLANES), pl.ds(floor_to(pos_ref[1, k], LANES), LANES)]
        return pltpu.make_async_copy(src, tiles.at[k], sems.at[k])

    def placed(tile, row, col, target, foreign):
        turned = pltpu.roll(tile, (target - col) & (LANES - 1), 1)
        code = (row & (SUBLANES - 1)) * LANES + target
        return cell == jnp.where(foreign == 0, code, -1), turned

    for k in range(STEPS):
        tile_copy(k).start()
    sums = [jnp.zeros((SUBLANES, LANES), jnp.float32) for _ in range(STEPS // FOLD)]
    for k in range(STEPS):
        base_row = pos_ref[0, k] + (HALF - row_id * SHARD)
        base_col = pos_ref[1, k] + HALF
        for l in range(k):
            row = base_row - pos_ref[0, l]
            col = base_col - pos_ref[1, l]
            foreign = (row >> 6) | (col >> 11)
            rows = pl.ds(pl.multiple_of(row & (SHARD - SUBLANES), SUBLANES), SUBLANES)
            cols = pl.ds(pl.multiple_of(col & (PATCH - LANES), LANES), LANES)
            here, turned = placed(psf_ref[rows, cols], row, col, STEPS * (k % FOLD) + l, foreign)
            sums[k // FOLD] = jnp.where(here, turned, sums[k // FOLD])
        if k % FOLD == FOLD - 1:
            wide[k // FOLD] = sums[k // FOLD]
    for k in range(STEPS):
        tile_copy(k).wait()
        local = pos_ref[0, k] - first
        here, turned = placed(tiles[k], local, pos_ref[1, k], STEPS * (k % FOLD) + k, local >> 5)
        wide[k // FOLD] = jnp.where(here, turned, wide[k // FOLD])
    for g in range(STEPS // FOLD):
        acc[g : g + 1, :] = jnp.sum(wide[g], axis=0, keepdims=True)
    out_ref[...] = jnp.broadcast_to(acc[...][None], (DEVICES, SUBLANES, LANES))


def table(pos, psf, residual):
    return pl.pallas_call(
        table_kernel,
        out_shape=jax.ShapeDtypeStruct((DEVICES, SUBLANES, LANES), jnp.float32),
        in_specs=[
            pl.BlockSpec(memory_space=pltpu.SMEM),
            pl.BlockSpec(memory_space=pltpu.VMEM),
            pl.BlockSpec(memory_space=pl.ANY),
        ],
        out_specs=pl.BlockSpec(memory_space=pltpu.VMEM),
        scratch_shapes=[
            pltpu.VMEM((STEPS, SUBLANES, LANES), jnp.float32),
            pltpu.VMEM((SUBLANES, SUBLANES, LANES), jnp.float32),
            pltpu.VMEM((SUBLANES, LANES), jnp.float32),
            pltpu.SemaphoreType.DMA((STEPS,)),
        ],
        name="table",
    )(pos, psf, residual)


def solve_kernel(parts_ref, out_ref, rows):
    chan_id = lax.axis_index("chan")
    per_chan = DEVICES // NCHAN
    for c in range(NCHAN):
        summed = parts_ref[c * per_chan]
        for d in range(1, per_chan):
            summed = summed + parts_ref[c * per_chan + d]
        for g in range(SUBLANES):
            rows[g, c : c + 1, :] = summed[g : g + 1, :]
            rows[g, NCHAN + c : NCHAN + c + 1, :] = jnp.zeros((1, LANES), jnp.float32)
    lane = lax.broadcasted_iota(jnp.int32, (SUBLANES, LANES), 1)
    sub = lax.broadcasted_iota(jnp.int32, (SUBLANES, LANES), 0)
    at = lane % STEPS
    group = lane // STEPS
    own = sub == chan_id
    amps = jnp.zeros((SUBLANES, LANES), jnp.float32)
    for k in range(STEPS):
        weights = jnp.where(at == k, -1.0, amps)
        products = jnp.where(group == k % FOLD, rows[k // FOLD] * weights, 0.0)
        value = -jnp.sum(products, axis=1, keepdims=True)
        total = jnp.sum(value, axis=0, keepdims=True)
        amp = jnp.broadcast_to(0.25 * (value + total / NCHAN), (SUBLANES, LANES))
        amps = jnp.where((at == k) & (sub < NCHAN), amp, amps)
        mine = jnp.sum(jnp.where(own, amp, 0.0), axis=0, keepdims=True)
        out_ref[k] = jnp.broadcast_to(mine, (SUBLANES, LANES))


def solve(parts):
    return pl.pallas_call(
        solve_kernel,
        out_shape=jax.ShapeDtypeStruct((STEPS, SUBLANES, LANES), jnp.float32),
        in_specs=[pl.BlockSpec(memory_space=pltpu.VMEM)],
        out_specs=pl.BlockSpec(memory_space=pltpu.VMEM),
        scratch_shapes=[pltpu.VMEM((SUBLANES, SUBLANES, LANES), jnp.float32)],
        name="solve",
    )(parts)


NEAR = (1, 2, 1, 2)
HALFWAY = (2, 0, 3, 1)


def place(z, y, c):
    return z * 8 + y * 2 + c


def needs(z, y, c, j):
    return 4 * z + y <= 2 * j + c <= 4 * z + y + 16


def near_held(z, y):
    return 4 * NEAR[z] + y


def halfway_held(z, y):
    return 4 * HALFWAY[z] + y if (y < 2) == (z % 2 == 0) else None


def turn(by, held):
    chips = [(z, y) for z in range(4) for y in range(4) if held(z, y) is not None]
    return [
        (place(z, y, c), place(z, (y + by) % 4, c))
        for z, y in chips
        for c in range(2)
        if needs(z, (y + by) % 4, c, held(z, y))
    ]


def climb(moves):
    return [(place(a, y, c), place(b, y, c)) for a, b in moves for y in range(4) for c in range(2)]


OUTER = climb([(1, 0), (2, 3)])
INNER = climb([(2, 1), (1, 2)])
ACROSS = [
    (place(HALFWAY[z], y, c), place(z, y, c))
    for z in range(4)
    for y in range(4)
    for c in range(2)
    if halfway_held(z, y) is not None
]


def permute(x, pairs):
    return lax.ppermute(x, ROWS, pairs)


def part_kernel(names, halves, late, from_residual, pos_ref, amps_ref, *rest):
    count = len(names)
    block_refs, rest = rest[:count], rest[count:]
    base_refs, rest = rest[: 1 if from_residual else len(halves)], rest[1 if from_residual else len(halves) :]
    out_refs, rest = rest[: len(halves)], rest[len(halves) :]
    images, (patch, sems, edge_sems) = rest[: len(halves)], rest[len(halves) :]
    z, y, c = (lax.axis_index(name) for name in ROWS)
    inner = (z == 1) | (z == 2)
    odd = z & 1
    near_slot = jnp.where(z == 0, 4, jnp.where(z == 1, 6, jnp.where(z == 2, 0, 2)))
    far_slot = jnp.where(odd == 0, 8, -2)
    lane = lax.broadcasted_iota(jnp.int32, (SUBLANES, LANES), 1)
    sub = lax.broadcasted_iota(jnp.int32, (SUBLANES, LANES), 0)

    def each_block(act):
        for i, (kind, by) in enumerate(names):
            source = (y - by) & 3
            if kind == "own":
                slot, held = 2 * z + source, None
            elif kind == "far":
                slot, held = far_slot + source, (source >> 1) == odd
            else:
                slot = near_slot + source
                held = None if kind == "near" else inner == (kind == "near_inner")
            slot = jnp.clip(slot, 0, SLOTS - 1)
            rows = pl.ds(pl.multiple_of(EDGE + slot * SHARD, SUBLANES), SHARD)
            copy = pltpu.make_async_copy(block_refs[i], patch.at[rows, :], sems.at[i])
            if held is None:
                act(copy)
            else:
                pl.when(held)(functools.partial(act, copy))

    each_block(lambda copy: copy.start())
    loads = []
    for n, image in enumerate(images):
        if from_residual and halves[n] == 1:
            image[...] = jnp.zeros(image.shape, jnp.float32)
        else:
            base = base_refs[0 if from_residual else n]
            loads.append(pltpu.make_async_copy(base, image.at[:, pl.ds(0, NCOL)], edge_sems.at[n]))
            loads[-1].start()
    each_block(lambda copy: copy.wait())
    for load in loads:
        load.wait()

    def peak(image, first, k):
        start = first - pos_ref[0, k] + HALF
        other = ((start >> 6) ^ c) & 1
        skew = (start & (SHARD - 1)) - other * SHARD
        slot = (((start >> 6) + other) >> 1) - 2 * z
        is_late = ((slot >> 1) == jnp.where(odd == 0, 4, 0)) | (slot == near_slot + ((y + 2) & 3))

        @pl.when((skew > -SLAB) & (is_late == late))
        def _():
            row = EDGE + slot * SHARD + skew
            off = row & (SUBLANES - 1)
            row = row - off
            left = pos_ref[1, k] - HALF
            shift = left & (LANES - 1)
            base = left - shift
            amp = amps_ref[k]
            carried = lane < shift
            upper = sub < SUBLANES - off
            groups = TALL // SUBLANES
            places = [sub + (g * SUBLANES + skew) for g in range(SLAB // SUBLANES)]
            within = [(at >= 0) & (at < SHARD) for at in places]
            before = [jnp.zeros((SUBLANES, LANES), jnp.float32)] * groups
            for t in range(PATCH // LANES + 1):
                if t < PATCH // LANES:
                    turned = []
                    for g in range(groups):
                        rows = pl.ds(pl.multiple_of(row + g * SUBLANES, SUBLANES), SUBLANES)
                        turned.append(pltpu.roll(patch[rows, pl.ds(t * LANES, LANES)], shift, 1))
                else:
                    turned = [jnp.zeros((SUBLANES, LANES), jnp.float32)] * groups
                back = (SUBLANES - off) & (SUBLANES - 1)
                joined = [pltpu.roll(jnp.where(carried, b, n), back, 0) for b, n in zip(before, turned)]
                cols = pl.ds(pl.multiple_of(base + t * LANES, LANES), LANES)
                for g in range(SLAB // SUBLANES):
                    rows = pl.ds(g * SUBLANES, SUBLANES)
                    value = jnp.where(within[g], jnp.where(upper, joined[g], joined[g + 1]), 0.0)
                    image[rows, cols] = image[rows, cols] - amp * value
                before = turned

    stores = []
    for n, image in enumerate(images):
        half = c if halves[n] == 0 else 1 - c
        first = (4 * z + y) * SHARD + half * SLAB
        lax.fori_loop(0, STEPS, lambda k, _, image=image, first=first: (peak(image, first, k), 0)[1], 0)
        stores.append(pltpu.make_async_copy(image.at[:, pl.ds(0, NCOL)], out_refs[n], edge_sems.at[n]))
        stores[-1].start()
    for store in stores:
        store.wait()


def part(names, halves, late, pos, amps, blocks, bases):
    anywhere = pl.BlockSpec(memory_space=pl.ANY)
    from_residual = not late
    return pl.pallas_call(
        functools.partial(part_kernel, names, halves, late, from_residual),
        out_shape=[jax.ShapeDtypeStruct((SLAB, NCOL), jnp.float32)] * len(halves),
        in_specs=[pl.BlockSpec(memory_space=pltpu.SMEM), pl.BlockSpec(memory_space=pltpu.VMEM)]
        + [anywhere] * (len(blocks) + len(bases)),
        out_specs=[anywhere] * len(halves),
        scratch_shapes=[pltpu.VMEM((SLAB, NCOL + LANES), jnp.float32)] * len(halves)
        + [
            pltpu.VMEM((2 * EDGE + SLOTS * SHARD, PATCH), jnp.float32),
            pltpu.SemaphoreType.DMA((len(names),)),
            pltpu.SemaphoreType.DMA((len(halves),)),
        ],
        compiler_params=pltpu.CompilerParams(vmem_limit_bytes=PART_VMEM),
    )(pos, amps, *blocks, *bases)


def join_kernel(mine_ref, other_ref, out_ref, *rest):
    piece_refs, (mine, other, sems, piece_sems) = rest[: len(PIECES)], rest[len(PIECES) :]
    chan_id = lax.axis_index("chan")

    def cols(ahead):
        return pl.ds(pl.multiple_of(((chan_id + ahead) & (NCHAN - 1)) * QUARTER, QUARTER), QUARTER)

    def load(ahead, n):
        src, dst = ((mine_ref, mine), (other_ref, other))[n]
        return pltpu.make_async_copy(src.at[:, cols(ahead)], dst.at[ahead], sems.at[n, ahead])

    order = (2, 1, 3, 0)
    for ahead in order:
        load(ahead, 0).start()
        load(ahead, 1).start()
    stores = []
    for ahead in order:
        load(ahead, 0).wait()
        load(ahead, 1).wait()
        mine[ahead] = mine[ahead] + other[ahead]
        stores.append(pltpu.make_async_copy(mine.at[ahead], out_ref.at[:, cols(ahead)], sems.at[2, ahead]))
        stores[-1].start()
        for i, (where, top, tall) in enumerate(PIECES):
            if where == ahead:
                src = mine.at[ahead, pl.ds(top, tall), :]
                stores.append(pltpu.make_async_copy(src, piece_refs[i], piece_sems.at[i]))
                stores[-1].start()
    for store in stores:
        store.wait()


def join(mine, other):
    anywhere = pl.BlockSpec(memory_space=pl.ANY)
    return pl.pallas_call(
        join_kernel,
        out_shape=[
            jax.ShapeDtypeStruct((SLAB, NCOL), jnp.float32),
            *(jax.ShapeDtypeStruct((tall, QUARTER), jnp.float32) for _, _, tall in PIECES),
        ],
        in_specs=[anywhere] * 2,
        out_specs=[anywhere] * (len(PIECES) + 1),
        scratch_shapes=[
            pltpu.VMEM((NCHAN, SLAB, QUARTER), jnp.float32),
            pltpu.VMEM((NCHAN, SLAB, QUARTER), jnp.float32),
            pltpu.SemaphoreType.DMA((3, NCHAN)),
            pltpu.SemaphoreType.DMA((len(PIECES),)),
        ],
        compiler_params=pltpu.CompilerParams(vmem_limit_bytes=JOIN_VMEM),
        name="join",
    )(mine, other)


def channel_sum(pieces):
    mine, right_top, right_low, far_top, far_low, left_top, left_low = pieces

    def shift(x, by):
        return lax.ppermute(x, "chan", [(i, (i + by) % NCHAN) for i in range(NCHAN)])

    far_top, far_low = shift(far_top, 1), shift(far_low, 3)
    from_left_low, from_right_top = shift(right_low, 1), shift(left_top, 3)
    from_left_top, from_right_low = shift(right_top + far_top, 1), shift(left_low + far_low, 3)
    return mine + jnp.concatenate([from_left_top + from_right_top, from_left_low + from_right_low], 0)


def cycle(residual, psf, positions):
    nrows = lax.axis_size(ROWS)
    slab, ncols = residual.shape[1:]
    z = lax.axis_index("rows_0")
    outer = (z == 0) | (z == 3)
    pos = positions.T
    own = psf[0]
    to_outer, to_inner = permute(own, OUTER), permute(own, INNER)
    own1, own3, own2 = (permute(own, turn(by, lambda z, y: 4 * z + y)) for by in (1, 3, 2))
    far = permute(own, ACROSS)
    parts = table(pos, own, residual[0])
    near = jnp.where(outer, to_outer, to_inner)
    near1, near3 = (permute(near, turn(by, near_held)) for by in (1, 3))
    parts, near = lax.optimization_barrier((parts, near))
    parts = lax.all_to_all(parts, CHAN_ROWS, 0, 0, tiled=True)
    far1, far2, far3 = (permute(far, turn(by, halfway_held)) for by in (1, 2, 3))
    near2_outer, near2_inner = permute(own2, OUTER), permute(own2, INNER)
    amps = solve(parts)
    early = (own, own1, own2, own3, near, near1, near3)
    mine, yours = part(EARLY, (0, 1), False, pos, amps, early, (residual[0],))
    rest = (near2_outer, near2_inner, far, far1, far2, far3)
    (yours,) = part(LATE, (1,), True, pos, amps, rest, (yours,))
    other = lax.ppermute(yours, "rows_2", [(0, 1), (1, 0)])
    (mine,) = part(LATE, (0,), True, pos, amps, rest, (mine,))
    image, *pieces = join(mine, other)
    summed = channel_sum(pieces)
    square = jnp.broadcast_to(jnp.sum(summed * summed), (DEVICES, 1, LANES))
    total = jnp.sum(lax.all_to_all(square, CHAN_ROWS, 0, 0, tiled=True)[:, 0, 0])
    count = slab * nrows * ncols
    normalized = summed * lax.rsqrt(total / count + 1e-06)
    return (image[None], normalized)


def solution(mesh):
    finer = Mesh(
        mesh.devices.reshape(mesh.shape["chan"], 4, 4, 2), ("chan", "rows_0", "rows_1", "rows_2")
    )
    return jax.shard_map(
        cycle,
        mesh=finer,
        in_specs=(P("chan", ROWS, None), P("chan", ROWS, None), P()),
        out_specs=(P("chan", ROWS, None), P(ROWS, "chan")),
        check_vma=False,
    )
```

profile of v0, /device:TPU:1, one launch (start us, length us, event | category | flops | bytes accessed | tf_op | source)
XLA Modules:
  0.0 164.4 jit_solution(14502893119921844284)
XLA Ops:
  0.6 1.3 collective-permute-start
  1.9 0.7 collective-permute-start.1
  2.6 1.3 collective-permute-start.2
  3.9 1.3 collective-permute-start.10
  5.2 7.3 %collective-permute-start.9 = (f32[64,2048]{1,0:T(8,128)}, f32[64,2048]{1,0:T(8,128)S(1)}, u32[]{:S(2)}, u32[]{:S(2)}) collective-permute-start(f32[64,2048]{1,0:T(8,128)} %bitcast.10), channel_id=1, source_target_pairs={{1,3},{2,4},{3,5},{4,6},{5,7},{6,0},{7,1},{8,10},{9,11},{10,12},{1... | collective-permute-start | bytes 1572872 | tf_op jit(solution)/shard_map/ppermute | solution.py:198
  12.5 3.2 %collective-permute-done = f32[64,2048]{1,0:T(8,128)S(1)} collective-permute-done((f32[64,2048]{1,0:T(8,128)}, f32[64,2048]{1,0:T(8,128)S(1)}, u32[]{:S(2)}, u32[]{:S(2)}) %collective-permute-start) | collective-permute-done | bytes 524320 | tf_op jit(solution)/shard_map/ppermute | solution.py:198
  15.7 1.3 collective-permute-start.5
  17.1 4.0 %collective-permute-start.11 = (f32[64,2048]{1,0:T(8,128)S(1)}, f32[64,2048]{1,0:T(8,128)S(1)}, u32[]{:S(2)}, u32[]{:S(2)}) collective-permute-start(f32[64,2048]{1,0:T(8,128)S(1)} %broadcast_select_fusion.rest_4_), channel_id=1, source_target_pairs={{0,2},{1,3},{2,4},{3,5},{4,6},{5,7},{6,0},{7,1},{8,10},{9,11},{10,... | collective-permute-start | bytes 1572872 | tf_op jit(solution)/shard_map/ppermute | solution.py:198
  21.1 6.9 %collective-permute-start.12 = (f32[64,2048]{1,0:T(8,128)S(1)}, f32[64,2048]{1,0:T(8,128)S(1)}, u32[]{:S(2)}, u32[]{:S(2)}) collective-permute-start(f32[64,2048]{1,0:T(8,128)S(1)} %broadcast_select_fusion.rest_4_), channel_id=1, source_target_pairs={{0,6},{1,7},{2,0},{3,1},{4,2},{5,3},{6,4},{7,5},{8,14},{9,15},{10,... | collective-permute-start | bytes 1572872 | tf_op jit(solution)/shard_map/ppermute | solution.py:198
  28.0 0.8 copy-done.3
  28.8 4.3 %collective-permute-done.5.rest_2_ = f32[64,2048]{1,0:T(8,128)S(1)} collective-permute-done((f32[64,2048]{1,0:T(8,128)}, f32[64,2048]{1,0:T(8,128)S(1)}, u32[]{:S(2)}, u32[]{:S(2)}) %collective-permute-start.5) | collective-permute-done | bytes 524320 | tf_op jit(solution)/shard_map/ppermute | solution.py:198
  33.0 2.3 %collective-permute-start.6 = (f32[64,2048]{1,0:T(8,128)S(1)}, f32[64,2048]{1,0:T(8,128)S(1)}, u32[]{:S(2)}, u32[]{:S(2)}) collective-permute-start(f32[64,2048]{1,0:T(8,128)S(1)} %collective-permute-done.5.rest_2_), channel_id=1, source_target_pairs={{0,2},{1,3},{2,4},{14,8},{15,9},{16,18},{17,19},{18,20},{30,24},{3... | collective-permute-start | bytes 1572872 | tf_op jit(solution)/shard_map/ppermute | solution.py:198
  35.4 0.8 copy-done.6
  36.2 2.1 %collective-permute-start.7 = (f32[64,2048]{1,0:T(8,128)S(1)}, f32[64,2048]{1,0:T(8,128)}, u32[]{:S(2)}, u32[]{:S(2)}) collective-permute-start(f32[64,2048]{1,0:T(8,128)S(1)} %collective-permute-done.5.rest_2_), channel_id=1, source_target_pairs={{0,4},{1,5},{2,6},{3,7},{12,8},{13,9},{14,10},{15,11},{16,20},{17,... | collective-permute-start | bytes 1572872 | tf_op jit(solution)/shard_map/ppermute | solution.py:198
  38.3 0.8 copy-done.8
  39.1 2.1 %collective-permute-start.8 = (f32[64,2048]{1,0:T(8,128)S(1)}, f32[64,2048]{1,0:T(8,128)}, u32[]{:S(2)}, u32[]{:S(2)}) collective-permute-start(f32[64,2048]{1,0:T(8,128)S(1)} %collective-permute-done.5.rest_2_), channel_id=1, source_target_pairs={{0,6},{1,7},{13,11},{14,12},{15,13},{16,22},{17,23},{29,27},{30,28... | collective-permute-start | bytes 1572872 | tf_op jit(solution)/shard_map/ppermute | solution.py:198
  41.2 1.5 collective-permute-done.11.rest_5_
  42.7 0.8 copy-done.10
  43.5 1.3 collective-permute-start.3
  44.8 0.8 copy-done.12
  45.6 1.5 collective-permute-start.4
  47.1 8.8 %table.1 = f32[128,8,128]{2,1,0:T(8,128)} custom-call(s32[2,32]{1,0:T(2,128)} %bitcast.14, f32[64,2048]{1,0:T(8,128)} %bitcast.12, f32[32,16384]{1,0:T(8,128)} %bitcast.4), custom_call_target="tpu_custom_call" | custom-call | tf_op jit(solution)/shard_map/table/pallas_call | solution.py:95
  55.9 37.6 %all_to_all.10.parts_ref = f32[128,8,128]{2,1,0:T(8,128)} all-to-all(f32[128,8,128]{2,1,0:T(8,128)} %table.1), channel_id=1, replica_groups=mesh['chan'=4,'rows_0'=4,'rows_1'=4,'rows_2'=2] {'chan','rows_0','rows_1..., dimensions={0} | all-to-all | bytes 1048576 | tf_op jit(solution)/shard_map/all_to_all | solution.py:393
  93.5 4.6 %solve.1.amps_ref = f32[32,8,128]{2,1,0:T(8,128)} custom-call(f32[128,8,128]{2,1,0:T(8,128)} %all_to_all.10.parts_ref), custom_call_target="tpu_custom_call" | custom-call | tf_op jit(solution)/shard_map/solve/pallas_call | solution.py:142
  98.1 0.9 copy-done.1
  99.0 1.0 copy-done.4
  100.0 1.0 copy-done.5
  101.1 1.0 copy-done.7
  102.1 1.0 copy-done.9
  103.2 1.0 copy-done.11
  104.2 1.0 copy-done.13
  105.2 9.8 %shard_map.50 = (f32[32,16384]{1,0:T(8,128)S(1)}, f32[32,16384]{1,0:T(8,128)S(1)}) custom-call(s32[2,32]{1,0:T(2,128)S(1)} %bitcast.15, f32[32,8,128]{2,1,0:T(8,128)S(1)} %copy-done.1, f32[64,2048]{1,0:T(8,128)S(1)} %bitcast.13, f32[64,2048]{1,0:T(8,128)S(1)} %copy-done.9, f32[64,2048]{1,0:T(8,128)} %collective-permute-done.2.rest_2_, ...), custom_call_target="tpu_custom_call" | custom-call | tf_op jit(solution)/shard_map/pallas_call | solution.py:299
  115.2 3.2 %shard_map.52 = f32[32,16384]{1,0:T(8,128)S(1)} custom-call(s32[2,32]{1,0:T(2,128)S(1)} %bitcast.16, f32[32,8,128]{2,1,0:T(8,128)S(1)} %copy-done.2, f32[64,2048]{1,0:T(8,128)} %collective-permute-done.3.rest_0_, f32[64,2048]{1,0:T(8,128)} %collective-permute-done.4.rest_1_, f32[64,2048]{1,0:T(8,128)S(1)} %collective-permute-done.5.rest_2_, ...), custom_call_target="tpu_custom_call" | custom-call | tf_op jit(solution)/shard_map/pallas_call | solution.py:299
  118.4 0.7 collective-permute-start.13
  119.0 3.2 %shard_map.51.mine_ref = f32[32,16384]{1,0:T(8,128)S(1)} custom-call(s32[2,32]{1,0:T(2,128)S(1)} %bitcast.17, f32[32,8,128]{2,1,0:T(8,128)S(1)} %copy-done.2, f32[64,2048]{1,0:T(8,128)} %collective-permute-done.3.rest_0_, f32[64,2048]{1,0:T(8,128)} %collective-permute-done.4.rest_1_, f32[64,2048]{1,0:T(8,128)S(1)} %collective-permute-done.5.rest_2_, ...), custom_call_target="tpu_custom_call" | custom-call | tf_op jit(solution)/shard_map/pallas_call | solution.py:299
  122.3 0.6 collective-permute-done.13.other_ref
  122.8 1.8 %join.1 = (f32[32,16384]{1,0:T(8,128)}, f32[32,4096]{1,0:T(8,128)S(1)}, f32[16,4096]{1,0:T(8,128)S(1)}, f32[16,4096]{1,0:T(8,128)S(1)}, f32[16,4096]{1,0:T(8,128...) custom-call(f32[32,16384]{1,0:T(8,128)S(1)} %shard_map.51.mine_ref, ...), custom_call_target="tpu_custom_call" | custom-call | tf_op jit(solution)/shard_map/join/pallas_call | solution.py:348
  125.0 2.4 %collective-permute-start.18 = (f32[16,4096]{1,0:T(8,128)S(1)}, f32[16,4096]{1,0:T(8,128)S(1)}, u32[]{:S(2)}, u32[]{:S(2)}) collective-permute-start(f32[16,4096]{1,0:T(8,128)S(1)} %get-tuple-element.25), channel_id=1, source_target_pairs={{0,96},{32,0},{64,32},{96,64},{1,97},{33,1},{65,33},{97,65},{2,98}... | collective-permute-start | bytes 786440 | tf_op jit(solution)/shard_map/ppermute | solution.py:371
  127.4 1.4 collective-permute-start.17
  128.9 4.6 %collective-permute-done.14 = f32[16,4096]{1,0:T(8,128)S(1)} collective-permute-done((f32[16,4096]{1,0:T(8,128)S(1)}, f32[16,4096]{1,0:T(8,128)S(1)}, u32[]{:S(2)}, u32[]{:S(2)}) %collective-permute-start.14) | collective-permute-done | bytes 262176 | tf_op jit(solution)/shard_map/ppermute | solution.py:371
  133.6 2.7 %collective-permute-start.19 = (f32[16,4096]{1,0:T(8,128)S(1)}, f32[16,4096]{1,0:T(8,128)S(1)}, u32[]{:S(2)}, u32[]{:S(2)}) collective-permute-start(f32[16,4096]{1,0:T(8,128)S(1)} %add.20), channel_id=1, source_target_pairs={{0,96},{32,0},{64,32},{96,64},{1,97},{33,1},{65,33},{97,65},{2,98}... | collective-permute-start | bytes 786440 | tf_op jit(solution)/shard_map/ppermute | solution.py:371
  136.3 1.7 %collective-permute-done.16 = f32[16,4096]{1,0:T(8,128)S(1)} collective-permute-done((f32[16,4096]{1,0:T(8,128)S(1)}, f32[16,4096]{1,0:T(8,128)S(1)}, u32[]{:S(2)}, u32[]{:S(2)}) %collective-permute-start.16) | collective-permute-done | bytes 262176 | tf_op jit(solution)/shard_map/ppermute | solution.py:371
  138.0 6.6 %collective-permute-done.15 = f32[16,4096]{1,0:T(8,128)S(1)} collective-permute-done((f32[16,4096]{1,0:T(8,128)S(1)}, f32[16,4096]{1,0:T(8,128)S(1)}, u32[]{:S(2)}, u32[]{:S(2)}) %collective-permute-start.15) | collective-permute-done | bytes 262176 | tf_op jit(solution)/shard_map/ppermute | solution.py:371
  144.8 0.7 multiply_reduce_fusion
  145.5 0.7 broadcast_in_dim.7
  146.2 16.0 %all_to_all.11 = f32[128,1,128]{2,1,0:T(1,128)S(1)} all-to-all(f32[128,1,128]{2,1,0:T(1,128)S(1)} %broadcast_in_dim.7), channel_id=1, replica_groups=mesh['chan'=4,'rows_0'=4,'rows_1'=4,'rows_2'=2] {'chan','rows_0','rows_1..., dimensions={0} | all-to-all | bytes 131072 | tf_op jit(solution)/shard_map/all_to_all | solution.py:406
  162.2 0.7 slice_reduce_fusion
  163.6 0.8 broadcast_multiply_fusion
  (39 shorter events, 0.7 us)
Async XLA Ops:
  0.6 15.1 %collective-permute-start = (f32[64,2048]{1,0:T(8,128)}, f32[64,2048]{1,0:T(8,128)S(1)}, u32[]{:S(2)}, u32[]{:S(2)}) collective-permute-start(f32[64,2048]{1,0:T(8,128)} %bitcast.6), channel_id=1, source_target_pairs={{8,0},{9,1},{10,2},{11,3},{12,4},{13,5},{14,6},{15,7},{16,24},{17,... | collective-permute-start | bytes 1572872 | tf_op jit(solution)/shard_map/ppermute | solution.py:198
  1.9 15.1 %collective-permute-start.1 = (f32[64,2048]{1,0:T(8,128)}, f32[64,2048]{1,0:T(8,128)S(1)}, u32[]{:S(2)}, u32[]{:S(2)}) collective-permute-start(f32[64,2048]{1,0:T(8,128)} %bitcast.7), channel_id=1, source_target_pairs={{16,8},{17,9},{18,10},{19,11},{20,12},{21,13},{22,14},{23,15},{8,1... | collective-permute-start | bytes 1572872 | tf_op jit(solution)/shard_map/ppermute | solution.py:198
  2.6 18.4 %collective-permute-start.2 = (f32[64,2048]{1,0:T(8,128)}, f32[64,2048]{1,0:T(8,128)}, u32[]{:S(2)}, u32[]{:S(2)}) collective-permute-start(f32[64,2048]{1,0:T(8,128)} %bitcast.8), channel_id=1, source_target_pairs={{3,7},{4,0},{5,1},{6,2},{7,3},{8,12},{9,13},{10,14},{11,15},{12,8}... | collective-permute-start | bytes 1572872 | tf_op jit(solution)/shard_map/ppermute | solution.py:198
  3.9 31.4 %collective-permute-start.10 = (f32[64,2048]{1,0:T(8,128)}, f32[64,2048]{1,0:T(8,128)S(1)}, u32[]{:S(2)}, u32[]{:S(2)}) collective-permute-start(f32[64,2048]{1,0:T(8,128)} %bitcast.9), channel_id=1, source_target_pairs={{2,0},{3,1},{4,2},{5,3},{6,4},{7,5},{8,14},{9,15},{10,8},{11,9},{1... | collective-permute-start | bytes 1572872 | tf_op jit(solution)/shard_map/ppermute | solution.py:198
  5.2 33.0 %collective-permute-start.9 = (f32[64,2048]{1,0:T(8,128)}, f32[64,2048]{1,0:T(8,128)S(1)}, u32[]{:S(2)}, u32[]{:S(2)}) collective-permute-start(f32[64,2048]{1,0:T(8,128)} %bitcast.10), channel_id=1, source_target_pairs={{1,3},{2,4},{3,5},{4,6},{5,7},{6,0},{7,1},{8,10},{9,11},{10,12},{1... | collective-permute-start | bytes 1572872 | tf_op jit(solution)/shard_map/ppermute | solution.py:198
  15.7 17.3 %collective-permute-start.5 = (f32[64,2048]{1,0:T(8,128)}, f32[64,2048]{1,0:T(8,128)S(1)}, u32[]{:S(2)}, u32[]{:S(2)}) collective-permute-start(f32[64,2048]{1,0:T(8,128)} %bitcast.11), channel_id=1, source_target_pairs={{16,0},{17,1},{18,2},{19,3},{4,12},{5,13},{6,14},{7,15},{24,16},{2... | collective-permute-start | bytes 1572872 | tf_op jit(solution)/shard_map/ppermute | solution.py:198
  17.1 25.7 %collective-permute-start.11 = (f32[64,2048]{1,0:T(8,128)S(1)}, f32[64,2048]{1,0:T(8,128)S(1)}, u32[]{:S(2)}, u32[]{:S(2)}) collective-permute-start(f32[64,2048]{1,0:T(8,128)S(1)} %broadcast_select_fusion.rest_4_), channel_id=1, source_target_pairs={{0,2},{1,3},{2,4},{3,5},{4,6},{5,7},{6,0},{7,1},{8,10},{9,11},{10,... | collective-permute-start | bytes 1572872 | tf_op jit(solution)/shard_map/ppermute | solution.py:198
  21.1 23.7 %collective-permute-start.12 = (f32[64,2048]{1,0:T(8,128)S(1)}, f32[64,2048]{1,0:T(8,128)S(1)}, u32[]{:S(2)}, u32[]{:S(2)}) collective-permute-start(f32[64,2048]{1,0:T(8,128)S(1)} %broadcast_select_fusion.rest_4_), channel_id=1, source_target_pairs={{0,6},{1,7},{2,0},{3,1},{4,2},{5,3},{6,4},{7,5},{8,14},{9,15},{10,... | collective-permute-start | bytes 1572872 | tf_op jit(solution)/shard_map/ppermute | solution.py:198
  27.9 0.8 copy-start.3
  33.0 82.1 %collective-permute-start.6 = (f32[64,2048]{1,0:T(8,128)S(1)}, f32[64,2048]{1,0:T(8,128)S(1)}, u32[]{:S(2)}, u32[]{:S(2)}) collective-permute-start(f32[64,2048]{1,0:T(8,128)S(1)} %collective-permute-done.5.rest_2_), channel_id=1, source_target_pairs={{0,2},{1,3},{2,4},{14,8},{15,9},{16,18},{17,19},{18,20},{30,24},{3... | collective-permute-start | bytes 1572872 | tf_op jit(solution)/shard_map/ppermute | solution.py:198
  35.4 0.8 copy-start.6
  36.2 78.9 %collective-permute-start.7 = (f32[64,2048]{1,0:T(8,128)S(1)}, f32[64,2048]{1,0:T(8,128)}, u32[]{:S(2)}, u32[]{:S(2)}) collective-permute-start(f32[64,2048]{1,0:T(8,128)S(1)} %collective-permute-done.5.rest_2_), channel_id=1, source_target_pairs={{0,4},{1,5},{2,6},{3,7},{12,8},{13,9},{14,10},{15,11},{16,20},{17,... | collective-permute-start | bytes 1572872 | tf_op jit(solution)/shard_map/ppermute | solution.py:198
  38.3 0.8 copy-start.8
  39.1 76.0 %collective-permute-start.8 = (f32[64,2048]{1,0:T(8,128)S(1)}, f32[64,2048]{1,0:T(8,128)}, u32[]{:S(2)}, u32[]{:S(2)}) collective-permute-start(f32[64,2048]{1,0:T(8,128)S(1)} %collective-permute-done.5.rest_2_), channel_id=1, source_target_pairs={{0,6},{1,7},{13,11},{14,12},{15,13},{16,22},{17,23},{29,27},{30,28... | collective-permute-start | bytes 1572872 | tf_op jit(solution)/shard_map/ppermute | solution.py:198
  42.7 0.8 copy-start.10
  43.5 71.6 %collective-permute-start.3 = (f32[64,2048]{1,0:T(8,128)}, f32[64,2048]{1,0:T(8,128)}, u32[]{:S(2)}, u32[]{:S(2)}) collective-permute-start(f32[64,2048]{1,0:T(8,128)} %collective-permute-done.2.rest_2_), channel_id=1, source_target_pairs={{8,0},{9,1},{10,2},{11,3},{12,4},{13,5},{14,6},{15,7},{16,24},{17,... | collective-permute-start | bytes 1572872 | tf_op jit(solution)/shard_map/ppermute | solution.py:198
  44.8 0.8 copy-start.12
  45.6 69.5 %collective-permute-start.4 = (f32[64,2048]{1,0:T(8,128)}, f32[64,2048]{1,0:T(8,128)}, u32[]{:S(2)}, u32[]{:S(2)}) collective-permute-start(f32[64,2048]{1,0:T(8,128)} %collective-permute-done.2.rest_2_), channel_id=1, source_target_pairs={{16,8},{17,9},{18,10},{19,11},{20,12},{21,13},{22,14},{23,15},{8,1... | collective-permute-start | bytes 1572872 | tf_op jit(solution)/shard_map/ppermute | solution.py:198
  47.1 51.0 %copy-start = (f32[1,32,16384]{2,1,0:T(8,128)S(1)}, f32[1,32,16384]{2,1,0:T(8,128)}, u32[]{:S(2)}) copy-start(f32[1,32,16384]{2,1,0:T(8,128)} %param.3) | copy-start | bytes 6291460
  47.1 51.0 %copy-start.14 = (s32[32,2]{0,1:T(2,128)S(1)}, s32[32,2]{0,1:T(2,128)}, u32[]{:S(2)}) copy-start(s32[32,2]{0,1:T(2,128)} %param.5) | copy-start | bytes 772
  98.1 0.9 copy-start.1
  99.0 1.0 copy-start.4
  100.0 1.0 copy-start.5
  101.1 1.0 copy-start.7
  102.1 1.0 copy-start.9
  103.2 1.0 copy-start.11
  104.2 1.0 copy-start.13
  105.2 9.9 %copy-start.2 = (f32[32,8,128]{2,1,0:T(8,128)S(1)}, f32[32,8,128]{2,1,0:T(8,128)}, u32[]{:S(2)}) copy-start(f32[32,8,128]{2,1,0:T(8,128)} %solve.1.amps_ref) | copy-start | bytes 393220
  118.4 4.5 %collective-permute-start.13 = (f32[32,16384]{1,0:T(8,128)S(1)}, f32[32,16384]{1,0:T(8,128)S(1)}, u32[]{:S(2)}, u32[]{:S(2)}) collective-permute-start(f32[32,16384]{1,0:T(8,128)S(1)} %shard_map.52), channel_id=1, source_target_pairs={{0,1},{1,0},{2,3},{3,2},{4,5},{5,4},{6,7},{7,6},{8,9},{9,8},{10,11... | collective-permute-start | bytes 6291464 | tf_op jit(solution)/shard_map/ppermute | solution.py:401
  124.7 8.8 %collective-permute-start.14 = (f32[16,4096]{1,0:T(8,128)S(1)}, f32[16,4096]{1,0:T(8,128)S(1)}, u32[]{:S(2)}, u32[]{:S(2)}) collective-permute-start(f32[16,4096]{1,0:T(8,128)S(1)} %get-tuple-element.21), channel_id=1, source_target_pairs={{0,32},{32,64},{64,96},{96,0},{1,33},{33,65},{65,97},{97,1},{2,34}... | collective-permute-start | bytes 786440 | tf_op jit(solution)/shard_map/ppermute | solution.py:371
  125.0 8.5 %collective-permute-start.18 = (f32[16,4096]{1,0:T(8,128)S(1)}, f32[16,4096]{1,0:T(8,128)S(1)}, u32[]{:S(2)}, u32[]{:S(2)}) collective-permute-start(f32[16,4096]{1,0:T(8,128)S(1)} %get-tuple-element.25), channel_id=1, source_target_pairs={{0,96},{32,0},{64,32},{96,64},{1,97},{33,1},{65,33},{97,65},{2,98}... | collective-permute-start | bytes 786440 | tf_op jit(solution)/shard_map/ppermute | solution.py:371
  127.4 10.6 %collective-permute-start.16 = (f32[16,4096]{1,0:T(8,128)S(1)}, f32[16,4096]{1,0:T(8,128)S(1)}, u32[]{:S(2)}, u32[]{:S(2)}) collective-permute-start(f32[16,4096]{1,0:T(8,128)S(1)} %get-tuple-element.22), channel_id=1, source_target_pairs={{0,96},{32,0},{64,32},{96,64},{1,97},{33,1},{65,33},{97,65},{2,98}... | collective-permute-start | bytes 786440 | tf_op jit(solution)/shard_map/ppermute | solution.py:371
  127.4 17.3 %collective-permute-start.17 = (f32[16,4096]{1,0:T(8,128)S(1)}, f32[16,4096]{1,0:T(8,128)S(1)}, u32[]{:S(2)}, u32[]{:S(2)}) collective-permute-start(f32[16,4096]{1,0:T(8,128)S(1)} %get-tuple-element.23), channel_id=1, source_target_pairs={{0,32},{32,64},{64,96},{96,0},{1,33},{33,65},{65,97},{97,1},{2,34}... | collective-permute-start | bytes 786440 | tf_op jit(solution)/shard_map/ppermute | solution.py:371
  133.5 11.2 %collective-permute-start.15 = (f32[16,4096]{1,0:T(8,128)S(1)}, f32[16,4096]{1,0:T(8,128)S(1)}, u32[]{:S(2)}, u32[]{:S(2)}) collective-permute-start(f32[16,4096]{1,0:T(8,128)S(1)} %add.18), channel_id=1, source_target_pairs={{0,32},{32,64},{64,96},{96,0},{1,33},{33,65},{65,97},{97,1},{2,34}... | collective-permute-start | bytes 786440 | tf_op jit(solution)/shard_map/ppermute | solution.py:371
  133.6 11.1 %collective-permute-start.19 = (f32[16,4096]{1,0:T(8,128)S(1)}, f32[16,4096]{1,0:T(8,128)S(1)}, u32[]{:S(2)}, u32[]{:S(2)}) collective-permute-start(f32[16,4096]{1,0:T(8,128)S(1)} %add.20), channel_id=1, source_target_pairs={{0,96},{32,0},{64,32},{96,64},{1,97},{33,1},{65,33},{97,65},{2,98}... | collective-permute-start | bytes 786440 | tf_op jit(solution)/shard_map/ppermute | solution.py:371
where the time goes:
time: 165 us; the launch traced here: 164 us
  blocking collectives  53.6 us (32%)
  starting transfers between devices  41 us (25%)
  Pallas kernels  31.5 us (19%)
  waiting for transfers between devices  22.5 us (14%)
  local copies, waits for them, and re-layouts  11.8 us (7%)
  other arithmetic  2.52 us (2%)
    all_to_all x1, blocking collectives, cycle(): parts = lax.all_to_all(parts, CHAN_ROWS, 0, 0, tiled=True)  37.6 us
    ppermute x13, starting transfers between devices, permute(): return lax.ppermute(x, ROWS, pairs)  33.3 us
    pallas_call x3, Pallas kernels, part(): pl.pallas_call(functools.partial(part_kernel, names, halves, late, from_r...  16.3 us
    all_to_all x1, blocking collectives, cycle(): lax.all_to_all(square, CHAN_ROWS, 0, 0, tiled=True)[:, 0, 0]  16 us
    ppermute x6, waiting for transfers between devices, shift(): lax.ppermute(x, 'chan', [(i, (i + by) % NCHAN) for i in range(NCHAN)])  12.9 us
    unnamed x30, local copies, waits for them, and re-layouts  11.1 us
    ppermute x13, waiting for transfers between devices, permute(): return lax.ppermute(x, ROWS, pairs)  8.99 us
    pallas_call x1, Pallas kernels, table(): pl.pallas_call(table_kernel, out_shape=jax.ShapeDtypeStruct((DEVICES, SUB...  8.77 us
  transfers between devices with their start and end apart: 20, of which 7 were waited for; matrix products, arithmetic and copies ran while one was open for 0% of the time, Pallas kernels for 16%

commit v1 on v0

--- a/solution.py
+++ b/solution.py
@@ -111,15 +111,15 @@
     )(pos, psf, residual)
 
 
-def solve_kernel(parts_ref, out_ref, rows):
+def solve(parts_ref, amps_ref, rows):
     chan_id = lax.axis_index("chan")
     per_chan = DEVICES // NCHAN
     for c in range(NCHAN):
-        summed = parts_ref[c * per_chan]
-        for d in range(1, per_chan):
-            summed = summed + parts_ref[c * per_chan + d]
+        sums = [parts_ref[c * per_chan + d] for d in range(per_chan)]
+        while len(sums) > 1:
+            sums = [a + b for a, b in zip(sums[::2], sums[1::2])]
         for g in range(SUBLANES):
-            rows[g, c : c + 1, :] = summed[g : g + 1, :]
+            rows[g, c : c + 1, :] = sums[0][g : g + 1, :]
             rows[g, NCHAN + c : NCHAN + c + 1, :] = jnp.zeros((1, LANES), jnp.float32)
     lane = lax.broadcasted_iota(jnp.int32, (SUBLANES, LANES), 1)
     sub = lax.broadcasted_iota(jnp.int32, (SUBLANES, LANES), 0)
@@ -135,18 +135,7 @@
         amp = jnp.broadcast_to(0.25 * (value + total / NCHAN), (SUBLANES, LANES))
         amps = jnp.where((at == k) & (sub < NCHAN), amp, amps)
         mine = jnp.sum(jnp.where(own, amp, 0.0), axis=0, keepdims=True)
-        out_ref[k] = jnp.broadcast_to(mine, (SUBLANES, LANES))
-
-
-def solve(parts):
-    return pl.pallas_call(
-        solve_kernel,
-        out_shape=jax.ShapeDtypeStruct((STEPS, SUBLANES, LANES), jnp.float32),
-        in_specs=[pl.BlockSpec(memory_space=pltpu.VMEM)],
-        out_specs=pl.BlockSpec(memory_space=pltpu.VMEM),
-        scratch_shapes=[pltpu.VMEM((SUBLANES, SUBLANES, LANES), jnp.float32)],
-        name="solve",
-    )(parts)
+        amps_ref[k] = jnp.broadcast_to(mine, (SUBLANES, LANES))
 
 
 NEAR = (1, 2, 1, 2)
@@ -194,11 +183,24 @@
 ]
 
 
+ACROSS_TWO = [
+    (place(HALFWAY[z], (y + 2) % 4, c), place(z, (y + 2) % 4, c))
+    for z in range(4)
+    for y in range(4)
+    for c in range(2)
+    if halfway_held(z, y) is not None and needs(z, (y + 2) % 4, c, halfway_held(z, y))
+]
+
+
 def permute(x, pairs):
     return lax.ppermute(x, ROWS, pairs)
 
 
 def part_kernel(names, halves, late, from_residual, pos_ref, amps_ref, *rest):
+    if from_residual:
+        parts_ref, (rest, parts, amps_rows, parts_sems) = amps_ref, (rest[:-3], *rest[-3:])
+        amps_ref = rest[len(names) + 1]
+        rest = (*rest[: len(names) + 1], *rest[len(names) + 2 :])
     count = len(names)
     block_refs, rest = rest[:count], rest[count:]
     base_refs, rest = rest[: 1 if from_residual else len(halves)], rest[1 if from_residual else len(halves) :]
@@ -230,6 +232,9 @@
             else:
                 pl.when(held)(functools.partial(act, copy))
 
+    if from_residual:
+        parts_load = pltpu.make_async_copy(parts_ref, parts, parts_sems.at[0])
+        parts_load.start()
     each_block(lambda copy: copy.start())
     loads = []
     for n, image in enumerate(images):
@@ -239,6 +244,9 @@
             base = base_refs[0 if from_residual else n]
             loads.append(pltpu.make_async_copy(base, image.at[:, pl.ds(0, NCOL)], edge_sems.at[n]))
             loads[-1].start()
+    if from_residual:
+        parts_load.wait()
+        solve(parts, amps_ref, amps_rows)
     each_block(lambda copy: copy.wait())
     for load in loads:
         load.wait()
@@ -264,21 +272,22 @@
             groups = TALL // SUBLANES
             places = [sub + (g * SUBLANES + skew) for g in range(SLAB // SUBLANES)]
             within = [(at >= 0) & (at < SHARD) for at in places]
-            before = [jnp.zeros((SUBLANES, LANES), jnp.float32)] * groups
+            back = (SUBLANES - off) & (SUBLANES - 1)
+            before = [jnp.zeros((SUBLANES, LANES), jnp.float32)] * (groups - 1)
             for t in range(PATCH // LANES + 1):
                 if t < PATCH // LANES:
-                    turned = []
+                    raised = []
                     for g in range(groups):
                         rows = pl.ds(pl.multiple_of(row + g * SUBLANES, SUBLANES), SUBLANES)
-                        turned.append(pltpu.roll(patch[rows, pl.ds(t * LANES, LANES)], shift, 1))
+                        raised.append(pltpu.roll(patch[rows, pl.ds(t * LANES, LANES)], back, 0))
+                    joined = [jnp.where(upper, raised[g], raised[g + 1]) for g in range(groups - 1)]
+                    turned = [pltpu.roll(x, shift, 1) for x in joined]
                 else:
-                    turned = [jnp.zeros((SUBLANES, LANES), jnp.float32)] * groups
-                back = (SUBLANES - off) & (SUBLANES - 1)
-                joined = [pltpu.roll(jnp.where(carried, b, n), back, 0) for b, n in zip(before, turned)]
+                    turned = [jnp.zeros((SUBLANES, LANES), jnp.float32)] * (groups - 1)
                 cols = pl.ds(pl.multiple_of(base + t * LANES, LANES), LANES)
-                for g in range(SLAB // SUBLANES):
+                for g in range(groups - 1):
                     rows = pl.ds(g * SUBLANES, SUBLANES)
-                    value = jnp.where(within[g], jnp.where(upper, joined[g], joined[g + 1]), 0.0)
+                    value = jnp.where(within[g], jnp.where(carried, before[g], turned[g]), 0.0)
                     image[rows, cols] = image[rows, cols] - amp * value
                 before = turned
 
@@ -295,19 +304,27 @@
 
 def part(names, halves, late, pos, amps, blocks, bases):
     anywhere = pl.BlockSpec(memory_space=pl.ANY)
-    from_residual = not late
+    vmem = pl.BlockSpec(memory_space=pltpu.VMEM)
+    images = [jax.ShapeDtypeStruct((SLAB, NCOL), jnp.float32)] * len(halves)
+    solved = [] if late else [jax.ShapeDtypeStruct((STEPS, SUBLANES, LANES), jnp.float32)]
+    solving = [
+        pltpu.VMEM((DEVICES, SUBLANES, LANES), jnp.float32),
+        pltpu.VMEM((SUBLANES, SUBLANES, LANES), jnp.float32),
+        pltpu.SemaphoreType.DMA((1,)),
+    ]
     return pl.pallas_call(
-        functools.partial(part_kernel, names, halves, late, from_residual),
-        out_shape=[jax.ShapeDtypeStruct((SLAB, NCOL), jnp.float32)] * len(halves),
-        in_specs=[pl.BlockSpec(memory_space=pltpu.SMEM), pl.BlockSpec(memory_space=pltpu.VMEM)]
+        functools.partial(part_kernel, names, halves, late, not late),
+        out_shape=solved + images,
+        in_specs=[pl.BlockSpec(memory_space=pltpu.SMEM), vmem if late else anywhere]
         + [anywhere] * (len(blocks) + len(bases)),
-        out_specs=[anywhere] * len(halves),
+        out_specs=[vmem] * len(solved) + [anywhere] * len(halves),
         scratch_shapes=[pltpu.VMEM((SLAB, NCOL + LANES), jnp.float32)] * len(halves)
         + [
             pltpu.VMEM((2 * EDGE + SLOTS * SHARD, PATCH), jnp.float32),
             pltpu.SemaphoreType.DMA((len(names),)),
             pltpu.SemaphoreType.DMA((len(halves),)),
-        ],
+        ]
+        + ([] if late else solving),
         compiler_params=pltpu.CompilerParams(vmem_limit_bytes=PART_VMEM),
     )(pos, amps, *blocks, *bases)
 
@@ -389,13 +406,12 @@
     parts = table(pos, own, residual[0])
     near = jnp.where(outer, to_outer, to_inner)
     near1, near3 = (permute(near, turn(by, near_held)) for by in (1, 3))
-    parts, near = lax.optimization_barrier((parts, near))
     parts = lax.all_to_all(parts, CHAN_ROWS, 0, 0, tiled=True)
-    far1, far2, far3 = (permute(far, turn(by, halfway_held)) for by in (1, 2, 3))
+    far1, far3 = (permute(far, turn(by, halfway_held)) for by in (1, 3))
+    far2 = permute(own2, ACROSS_TWO)
     near2_outer, near2_inner = permute(own2, OUTER), permute(own2, INNER)
-    amps = solve(parts)
     early = (own, own1, own2, own3, near, near1, near3)
-    mine, yours = part(EARLY, (0, 1), False, pos, amps, early, (residual[0],))
+    amps, mine, yours = part(EARLY, (0, 1), False, pos, parts, early, (residual[0],))
     rest = (near2_outer, near2_inner, far, far1, far2, far3)
     (yours,) = part(LATE, (1,), True, pos, amps, rest, (yours,))
     other = lax.ppermute(yours, "rows_2", [(0, 1), (1, 0)])

time: 165 us -> 151 us (0.915)
  blocking collectives: 53.6 us -> 35.2 us
  starting transfers between devices: 41 us -> 47 us
  Pallas kernels: 31.5 us -> 28.4 us
  waiting for transfers between devices: 22.5 us -> 25.1 us
    all_to_all x1, blocking collectives: 37.6 us -> 21 us  [cycle(): parts = lax.all_to_all(parts, CHAN_ROWS, 0, 0, tiled=True)]
    ppermute x13, starting transfers between devices: 33.3 us -> 39.8 us  [permute(): return lax.ppermute(x, ROWS, pairs)]
    pallas_call x4 -> x3, Pallas kernels: 20.9 us -> 17.8 us  [part(): pl.pallas_call(functools.partial(part_kernel, names, halves, late, not la...]
    all_to_all x1, blocking collectives: 16 us -> 14.2 us  [cycle(): lax.all_to_all(square, CHAN_ROWS, 0, 0, tiled=True)[:, 0, 0]]
    unnamed x30 -> x26, local copies, waits for them, and re-layouts: 11.1 us -> 10.2 us
where the time goes in v1:
time: 151 us
  starting transfers between devices  47 us (31%)
  blocking collectives  35.2 us (23%)
  Pallas kernels  28.4 us (19%)
  waiting for transfers between devices  25.1 us (17%)
  local copies, waits for them, and re-layouts  10.9 us (7%)
  other arithmetic  2.52 us (2%)
  between operations  1.59 us (1%)
    ppermute x13, starting transfers between devices, permute(): return lax.ppermute(x, ROWS, pairs)  39.8 us
    all_to_all x1, blocking collectives, cycle(): parts = lax.all_to_all(parts, CHAN_ROWS, 0, 0, tiled=True)  21 us
    pallas_call x3, Pallas kernels, part(): pl.pallas_call(functools.partial(part_kernel, names, halves, late, not la...  17.8 us
    all_to_all x1, blocking collectives, cycle(): lax.all_to_all(square, CHAN_ROWS, 0, 0, tiled=True)[:, 0, 0]  14.2 us
    ppermute x6, waiting for transfers between devices, shift(): lax.ppermute(x, 'chan', [(i, (i + by) % NCHAN) for i in range(NCHAN)])  14 us
    ppermute x13, waiting for transfers between devices, permute(): return lax.ppermute(x, ROWS, pairs)  10.4 us
    unnamed x26, local copies, waits for them, and re-layouts  10.2 us
    pallas_call x1, Pallas kernels, table(): pl.pallas_call(table_kernel, out_shape=jax.ShapeDtypeStruct((DEVICES, SUB...  8.77 us
  transfers between devices with their start and end apart: 20, of which 7 were waited for; matrix products, arithmetic and copies ran while one was open for 0% of the time, Pallas kernels for 16%

profile of v1, /device:TPU:1, one launch (start us, length us, event | category | flops | bytes accessed | tf_op | source)
XLA Modules:
  0.0 150.6 jit_solution(15678024400013420011)
XLA Ops:
  0.6 1.3 collective-permute-start.3
  1.9 0.7 collective-permute-start.4
  2.6 4.0 %collective-permute-start = (f32[64,2048]{1,0:T(8,128)}, f32[64,2048]{1,0:T(8,128)S(1)}, u32[]{:S(2)}, u32[]{:S(2)}) collective-permute-start(f32[64,2048]{1,0:T(8,128)} %bitcast.8), channel_id=1, source_target_pairs={{1,3},{2,4},{3,5},{4,6},{5,7},{6,0},{7,1},{8,10},{9,11},{10,12},{1... | collective-permute-start | bytes 1572872 | tf_op jit(solution)/shard_map/ppermute | solution.py:196
  6.7 1.3 collective-permute-start.1
  8.0 1.3 collective-permute-start.2
  9.3 6.3 %collective-permute-done.3 = f32[64,2048]{1,0:T(8,128)S(1)} collective-permute-done((f32[64,2048]{1,0:T(8,128)}, f32[64,2048]{1,0:T(8,128)S(1)}, u32[]{:S(2)}, u32[]{:S(2)}) %collective-permute-start.3) | collective-permute-done | bytes 524320 | tf_op jit(solution)/shard_map/ppermute | solution.py:196
  15.6 1.3 collective-permute-start.9
  16.9 4.1 %collective-permute-start.5 = (f32[64,2048]{1,0:T(8,128)S(1)}, f32[64,2048]{1,0:T(8,128)S(1)}, u32[]{:S(2)}, u32[]{:S(2)}) collective-permute-start(f32[64,2048]{1,0:T(8,128)S(1)} %broadcast_select_fusion.rest_4_), channel_id=1, source_target_pairs={{0,2},{1,3},{2,4},{3,5},{4,6},{5,7},{6,0},{7,1},{8,10},{9,11},{10,... | collective-permute-start | bytes 1572872 | tf_op jit(solution)/shard_map/ppermute | solution.py:196
  21.1 0.8 copy-done.4
  21.8 5.5 %collective-permute-start.6 = (f32[64,2048]{1,0:T(8,128)S(1)}, f32[64,2048]{1,0:T(8,128)S(1)}, u32[]{:S(2)}, u32[]{:S(2)}) collective-permute-start(f32[64,2048]{1,0:T(8,128)S(1)} %broadcast_select_fusion.rest_4_), channel_id=1, source_target_pairs={{0,6},{1,7},{2,0},{3,1},{4,2},{5,3},{6,4},{7,5},{8,14},{9,15},{10,... | collective-permute-start | bytes 1572872 | tf_op jit(solution)/shard_map/ppermute | solution.py:196
  27.4 0.8 copy-done.1
  28.2 4.0 %collective-permute-done.1.rest_2_ = f32[64,2048]{1,0:T(8,128)} collective-permute-done((f32[64,2048]{1,0:T(8,128)}, f32[64,2048]{1,0:T(8,128)}, u32[]{:S(2)}, u32[]{:S(2)}) %collective-permute-start.1) | collective-permute-done | bytes 524320 | tf_op jit(solution)/shard_map/ppermute | solution.py:196
  32.2 1.3 collective-permute-start.7
  33.5 0.8 copy-done.6
  34.3 1.5 collective-permute-start.8
  35.8 9.7 %collective-permute-start.11 = (f32[64,2048]{1,0:T(8,128)}, f32[64,2048]{1,0:T(8,128)}, u32[]{:S(2)}, u32[]{:S(2)}) collective-permute-start(f32[64,2048]{1,0:T(8,128)} %collective-permute-done.1.rest_2_), channel_id=1, source_target_pairs={{20,4},{21,5},{22,6},{23,7},{0,8},{1,9},{2,10},{3,11},{28,20},{29,... | collective-permute-start | bytes 1572872 | tf_op jit(solution)/shard_map/ppermute | solution.py:196
  45.4 0.8 copy-done.8
  46.2 5.9 %collective-permute-start.10 = (f32[64,2048]{1,0:T(8,128)S(1)}, f32[64,2048]{1,0:T(8,128)}, u32[]{:S(2)}, u32[]{:S(2)}) collective-permute-start(f32[64,2048]{1,0:T(8,128)S(1)} %collective-permute-done.9.rest_2_), channel_id=1, source_target_pairs={{0,2},{1,3},{2,4},{14,8},{15,9},{16,18},{17,19},{18,20},{30,24},{3... | collective-permute-start | bytes 1572872 | tf_op jit(solution)/shard_map/ppermute | solution.py:196
  52.1 0.8 copy-done.10
  52.9 2.1 %collective-permute-start.12 = (f32[64,2048]{1,0:T(8,128)S(1)}, f32[64,2048]{1,0:T(8,128)}, u32[]{:S(2)}, u32[]{:S(2)}) collective-permute-start(f32[64,2048]{1,0:T(8,128)S(1)} %collective-permute-done.9.rest_2_), channel_id=1, source_target_pairs={{0,6},{1,7},{13,11},{14,12},{15,13},{16,22},{17,23},{29,27},{30,28... | collective-permute-start | bytes 1572872 | tf_op jit(solution)/shard_map/ppermute | solution.py:196
  55.0 8.8 %table.1 = f32[128,8,128]{2,1,0:T(8,128)} custom-call(s32[2,32]{1,0:T(2,128)} %bitcast.14, f32[64,2048]{1,0:T(8,128)} %bitcast.12, f32[32,16384]{1,0:T(8,128)} %bitcast.4), custom_call_target="tpu_custom_call" | custom-call | tf_op jit(solution)/shard_map/table/pallas_call | solution.py:95
  63.8 21.0 %all_to_all.10.amps_ref = f32[128,8,128]{2,1,0:T(8,128)S(1)} all-to-all(f32[128,8,128]{2,1,0:T(8,128)} %table.1), channel_id=1, replica_groups=mesh['chan'=4,'rows_0'=4,'rows_1'=4,'rows_2'=2] {'chan','rows_0','rows_1..., dimensions={0} | all-to-all | bytes 1048576 | tf_op jit(solution)/shard_map/all_to_all | solution.py:409
  84.7 1.0 copy-done.2
  85.8 1.0 copy-done.3
  86.8 1.0 copy-done.5
  87.9 1.0 copy-done.7
  88.9 1.0 copy-done.9
  89.9 1.0 copy-done.11
  91.0 11.6 %shard_map.50 = (f32[32,8,128]{2,1,0:T(8,128)S(1)}, f32[32,16384]{1,0:T(8,128)S(1)}, f32[32,16384]{1,0:T(8,128)S(1)}) custom-call(s32[2,32]{1,0:T(2,128)S(1)} %bitcast.15, f32[128,8,128]{2,1,0:T(8,128)S(1)} %all_to_all.10.amps_ref, f32[64,2048]{1,0:T(8,128)S(1)} %bitcast.13, f32[64,2048]{1,0:T(8,128)S(1)} %copy-done.5, ...), custom_call_target="tpu_custom_call" | custom-call | tf_op jit(solution)/shard_map/pallas_call | solution.py:315
  102.7 3.1 %shard_map.52 = f32[32,16384]{1,0:T(8,128)S(1)} custom-call(s32[2,32]{1,0:T(2,128)S(1)} %bitcast.16, f32[32,8,128]{2,1,0:T(8,128)S(1)} %get-tuple-element.13.amps_ref, f32[64,2048]{1,0:T(8,128)S(1)} %collective-permute-done.7.rest_0_, f32[64,2048]{1,0:T(8,128)} %collective-permute-done.8.rest_1_, f32[64,2048]{1,0:T(8,128)S(1)} %collective-permute-done.9.rest_2_, ...), custom_call_target="tpu_custom_call" | custom-call | tf_op jit(solution)/shard_map/pallas_call | solution.py:315
  105.8 0.7 collective-permute-start.13
  106.5 3.1 %shard_map.51.mine_ref = f32[32,16384]{1,0:T(8,128)S(1)} custom-call(s32[2,32]{1,0:T(2,128)S(1)} %bitcast.17, f32[32,8,128]{2,1,0:T(8,128)S(1)} %get-tuple-element.13.amps_ref, f32[64,2048]{1,0:T(8,128)S(1)} %collective-permute-done.7.rest_0_, f32[64,2048]{1,0:T(8,128)} %collective-permute-done.8.rest_1_, f32[64,2048]{1,0:T(8,128)S(1)} %collective-permute-done.9.rest_2_, ...), custom_call_target="tpu_custom_call" | custom-call | tf_op jit(solution)/shard_map/pallas_call | solution.py:315
  109.6 0.7 collective-permute-done.13.other_ref
  110.3 1.8 %join.1 = (f32[32,16384]{1,0:T(8,128)}, f32[32,4096]{1,0:T(8,128)S(1)}, f32[16,4096]{1,0:T(8,128)S(1)}, f32[16,4096]{1,0:T(8,128)S(1)}, f32[16,4096]{1,0:T(8,128...) custom-call(f32[32,16384]{1,0:T(8,128)S(1)} %shard_map.51.mine_ref, ...), custom_call_target="tpu_custom_call" | custom-call | tf_op jit(solution)/shard_map/join/pallas_call | solution.py:365
  112.1 0.9 collective-permute-start.18
  113.0 0.6 collective-permute-start.14
  113.6 0.3 collective-permute-start.17
  113.9 2.4 %collective-permute-start.16 = (f32[16,4096]{1,0:T(8,128)S(1)}, f32[16,4096]{1,0:T(8,128)S(1)}, u32[]{:S(2)}, u32[]{:S(2)}) collective-permute-start(f32[16,4096]{1,0:T(8,128)S(1)} %get-tuple-element.20), channel_id=1, source_target_pairs={{0,96},{32,0},{64,32},{96,64},{1,97},{33,1},{65,33},{97,65},{2,98}... | collective-permute-start | bytes 786440 | tf_op jit(solution)/shard_map/ppermute | solution.py:388
  116.3 3.3 %collective-permute-done.18 = f32[16,4096]{1,0:T(8,128)S(1)} collective-permute-done((f32[16,4096]{1,0:T(8,128)S(1)}, f32[16,4096]{1,0:T(8,128)S(1)}, u32[]{:S(2)}, u32[]{:S(2)}) %collective-permute-start.18) | collective-permute-done | bytes 262176 | tf_op jit(solution)/shard_map/ppermute | solution.py:388
  119.7 2.1 %collective-permute-start.19 = (f32[16,4096]{1,0:T(8,128)S(1)}, f32[16,4096]{1,0:T(8,128)S(1)}, u32[]{:S(2)}, u32[]{:S(2)}) collective-permute-start(f32[16,4096]{1,0:T(8,128)S(1)} %add.20), channel_id=1, source_target_pairs={{0,96},{32,0},{64,32},{96,64},{1,97},{33,1},{65,33},{97,65},{2,98}... | collective-permute-start | bytes 786440 | tf_op jit(solution)/shard_map/ppermute | solution.py:388
  122.0 5.1 %collective-permute-done.17 = f32[16,4096]{1,0:T(8,128)S(1)} collective-permute-done((f32[16,4096]{1,0:T(8,128)S(1)}, f32[16,4096]{1,0:T(8,128)S(1)}, u32[]{:S(2)}, u32[]{:S(2)}) %collective-permute-start.17) | collective-permute-done | bytes 262176 | tf_op jit(solution)/shard_map/ppermute | solution.py:388
  127.1 3.8 %collective-permute-done.19 = f32[16,4096]{1,0:T(8,128)S(1)} collective-permute-done((f32[16,4096]{1,0:T(8,128)S(1)}, f32[16,4096]{1,0:T(8,128)S(1)}, u32[]{:S(2)}, u32[]{:S(2)}) %collective-permute-start.19) | collective-permute-done | bytes 262176 | tf_op jit(solution)/shard_map/ppermute | solution.py:388
  130.9 1.8 %collective-permute-done.15 = f32[16,4096]{1,0:T(8,128)S(1)} collective-permute-done((f32[16,4096]{1,0:T(8,128)S(1)}, f32[16,4096]{1,0:T(8,128)S(1)}, u32[]{:S(2)}, u32[]{:S(2)}) %collective-permute-start.15) | collective-permute-done | bytes 262176 | tf_op jit(solution)/shard_map/ppermute | solution.py:388
  132.7 0.7 multiply_reduce_fusion
  133.5 0.7 broadcast_in_dim.7
  134.2 14.2 %all_to_all.11 = f32[128,1,128]{2,1,0:T(1,128)S(1)} all-to-all(f32[128,1,128]{2,1,0:T(1,128)S(1)} %broadcast_in_dim.7), channel_id=1, replica_groups=mesh['chan'=4,'rows_0'=4,'rows_1'=4,'rows_2'=2] {'chan','rows_0','rows_1..., dimensions={0} | all-to-all | bytes 131072 | tf_op jit(solution)/shard_map/all_to_all | solution.py:422
  148.3 0.7 slice_reduce_fusion
  149.8 0.8 broadcast_multiply_fusion
  (34 shorter events, 0.3 us)
Async XLA Ops:
  0.6 15.0 %collective-permute-start.3 = (f32[64,2048]{1,0:T(8,128)}, f32[64,2048]{1,0:T(8,128)S(1)}, u32[]{:S(2)}, u32[]{:S(2)}) collective-permute-start(f32[64,2048]{1,0:T(8,128)} %bitcast.6), channel_id=1, source_target_pairs={{8,0},{9,1},{10,2},{11,3},{12,4},{13,5},{14,6},{15,7},{16,24},{17,... | collective-permute-start | bytes 1572872 | tf_op jit(solution)/shard_map/ppermute | solution.py:196
  1.9 14.9 %collective-permute-start.4 = (f32[64,2048]{1,0:T(8,128)}, f32[64,2048]{1,0:T(8,128)S(1)}, u32[]{:S(2)}, u32[]{:S(2)}) collective-permute-start(f32[64,2048]{1,0:T(8,128)} %bitcast.7), channel_id=1, source_target_pairs={{16,8},{17,9},{18,10},{19,11},{20,12},{21,13},{22,14},{23,15},{8,1... | collective-permute-start | bytes 1572872 | tf_op jit(solution)/shard_map/ppermute | solution.py:196
  2.6 18.4 %collective-permute-start = (f32[64,2048]{1,0:T(8,128)}, f32[64,2048]{1,0:T(8,128)S(1)}, u32[]{:S(2)}, u32[]{:S(2)}) collective-permute-start(f32[64,2048]{1,0:T(8,128)} %bitcast.8), channel_id=1, source_target_pairs={{1,3},{2,4},{3,5},{4,6},{5,7},{6,0},{7,1},{8,10},{9,11},{10,12},{1... | collective-permute-start | bytes 1572872 | tf_op jit(solution)/shard_map/ppermute | solution.py:196
  6.7 25.5 %collective-permute-start.1 = (f32[64,2048]{1,0:T(8,128)}, f32[64,2048]{1,0:T(8,128)}, u32[]{:S(2)}, u32[]{:S(2)}) collective-permute-start(f32[64,2048]{1,0:T(8,128)} %bitcast.9), channel_id=1, source_target_pairs={{3,7},{4,0},{5,1},{6,2},{7,3},{8,12},{9,13},{10,14},{11,15},{12,8}... | collective-permute-start | bytes 1572872 | tf_op jit(solution)/shard_map/ppermute | solution.py:196
  8.0 25.5 %collective-permute-start.2 = (f32[64,2048]{1,0:T(8,128)}, f32[64,2048]{1,0:T(8,128)S(1)}, u32[]{:S(2)}, u32[]{:S(2)}) collective-permute-start(f32[64,2048]{1,0:T(8,128)} %bitcast.10), channel_id=1, source_target_pairs={{2,0},{3,1},{4,2},{5,3},{6,4},{7,5},{8,14},{9,15},{10,8},{11,9},{1... | collective-permute-start | bytes 1572872 | tf_op jit(solution)/shard_map/ppermute | solution.py:196
  15.6 20.2 %collective-permute-start.9 = (f32[64,2048]{1,0:T(8,128)}, f32[64,2048]{1,0:T(8,128)S(1)}, u32[]{:S(2)}, u32[]{:S(2)}) collective-permute-start(f32[64,2048]{1,0:T(8,128)} %bitcast.11), channel_id=1, source_target_pairs={{16,0},{17,1},{18,2},{19,3},{4,12},{5,13},{6,14},{7,15},{24,16},{2... | collective-permute-start | bytes 1572872 | tf_op jit(solution)/shard_map/ppermute | solution.py:196
  16.9 28.5 %collective-permute-start.5 = (f32[64,2048]{1,0:T(8,128)S(1)}, f32[64,2048]{1,0:T(8,128)S(1)}, u32[]{:S(2)}, u32[]{:S(2)}) collective-permute-start(f32[64,2048]{1,0:T(8,128)S(1)} %broadcast_select_fusion.rest_4_), channel_id=1, source_target_pairs={{0,2},{1,3},{2,4},{3,5},{4,6},{5,7},{6,0},{7,1},{8,10},{9,11},{10,... | collective-permute-start | bytes 1572872 | tf_op jit(solution)/shard_map/ppermute | solution.py:196
  21.1 0.8 copy-start.4
  21.8 30.2 %collective-permute-start.6 = (f32[64,2048]{1,0:T(8,128)S(1)}, f32[64,2048]{1,0:T(8,128)S(1)}, u32[]{:S(2)}, u32[]{:S(2)}) collective-permute-start(f32[64,2048]{1,0:T(8,128)S(1)} %broadcast_select_fusion.rest_4_), channel_id=1, source_target_pairs={{0,6},{1,7},{2,0},{3,1},{4,2},{5,3},{6,4},{7,5},{8,14},{9,15},{10,... | collective-permute-start | bytes 1572872 | tf_op jit(solution)/shard_map/ppermute | solution.py:196
  27.4 0.8 copy-start.1
  32.2 70.4 %collective-permute-start.7 = (f32[64,2048]{1,0:T(8,128)}, f32[64,2048]{1,0:T(8,128)S(1)}, u32[]{:S(2)}, u32[]{:S(2)}) collective-permute-start(f32[64,2048]{1,0:T(8,128)} %collective-permute-done.1.rest_2_), channel_id=1, source_target_pairs={{8,0},{9,1},{10,2},{11,3},{12,4},{13,5},{14,6},{15,7},{16,24},{17,... | collective-permute-start | bytes 1572872 | tf_op jit(solution)/shard_map/ppermute | solution.py:196
  33.5 0.8 copy-start.6
  34.3 68.3 %collective-permute-start.8 = (f32[64,2048]{1,0:T(8,128)}, f32[64,2048]{1,0:T(8,128)}, u32[]{:S(2)}, u32[]{:S(2)}) collective-permute-start(f32[64,2048]{1,0:T(8,128)} %collective-permute-done.1.rest_2_), channel_id=1, source_target_pairs={{16,8},{17,9},{18,10},{19,11},{20,12},{21,13},{22,14},{23,15},{8,1... | collective-permute-start | bytes 1572872 | tf_op jit(solution)/shard_map/ppermute | solution.py:196
  35.8 66.9 %collective-permute-start.11 = (f32[64,2048]{1,0:T(8,128)}, f32[64,2048]{1,0:T(8,128)}, u32[]{:S(2)}, u32[]{:S(2)}) collective-permute-start(f32[64,2048]{1,0:T(8,128)} %collective-permute-done.1.rest_2_), channel_id=1, source_target_pairs={{20,4},{21,5},{22,6},{23,7},{0,8},{1,9},{2,10},{3,11},{28,20},{29,... | collective-permute-start | bytes 1572872 | tf_op jit(solution)/shard_map/ppermute | solution.py:196
  45.4 0.8 copy-start.8
  46.2 56.4 %collective-permute-start.10 = (f32[64,2048]{1,0:T(8,128)S(1)}, f32[64,2048]{1,0:T(8,128)}, u32[]{:S(2)}, u32[]{:S(2)}) collective-permute-start(f32[64,2048]{1,0:T(8,128)S(1)} %collective-permute-done.9.rest_2_), channel_id=1, source_target_pairs={{0,2},{1,3},{2,4},{14,8},{15,9},{16,18},{17,19},{18,20},{30,24},{3... | collective-permute-start | bytes 1572872 | tf_op jit(solution)/shard_map/ppermute | solution.py:196
  52.1 0.8 copy-start.10
  52.9 49.8 %collective-permute-start.12 = (f32[64,2048]{1,0:T(8,128)S(1)}, f32[64,2048]{1,0:T(8,128)}, u32[]{:S(2)}, u32[]{:S(2)}) collective-permute-start(f32[64,2048]{1,0:T(8,128)S(1)} %collective-permute-done.9.rest_2_), channel_id=1, source_target_pairs={{0,6},{1,7},{13,11},{14,12},{15,13},{16,22},{17,23},{29,27},{30,28... | collective-permute-start | bytes 1572872 | tf_op jit(solution)/shard_map/ppermute | solution.py:196
  55.0 29.7 %copy-start = (f32[1,32,16384]{2,1,0:T(8,128)S(1)}, f32[1,32,16384]{2,1,0:T(8,128)}, u32[]{:S(2)}) copy-start(f32[1,32,16384]{2,1,0:T(8,128)} %param.3) | copy-start | bytes 6291460
  55.0 29.7 %copy-start.12 = (s32[32,2]{0,1:T(2,128)S(1)}, s32[32,2]{0,1:T(2,128)}, u32[]{:S(2)}) copy-start(s32[32,2]{0,1:T(2,128)} %param.5) | copy-start | bytes 772
  84.7 1.0 copy-start.2
  85.8 1.0 copy-start.3
  86.8 1.0 copy-start.5
  87.8 1.0 copy-start.7
  88.9 1.0 copy-start.9
  89.9 1.0 copy-start.11
  105.8 4.5 %collective-permute-start.13 = (f32[32,16384]{1,0:T(8,128)S(1)}, f32[32,16384]{1,0:T(8,128)S(1)}, u32[]{:S(2)}, u32[]{:S(2)}) collective-permute-start(f32[32,16384]{1,0:T(8,128)S(1)} %shard_map.52), channel_id=1, source_target_pairs={{0,1},{1,0},{2,3},{3,2},{4,5},{5,4},{6,7},{7,6},{8,9},{9,8},{10,11... | collective-permute-start | bytes 6291464 | tf_op jit(solution)/shard_map/ppermute | solution.py:417
  112.1 7.6 %collective-permute-start.18 = (f32[16,4096]{1,0:T(8,128)S(1)}, f32[16,4096]{1,0:T(8,128)S(1)}, u32[]{:S(2)}, u32[]{:S(2)}) collective-permute-start(f32[16,4096]{1,0:T(8,128)S(1)} %get-tuple-element.23), channel_id=1, source_target_pairs={{0,96},{32,0},{64,32},{96,64},{1,97},{33,1},{65,33},{97,65},{2,98}... | collective-permute-start | bytes 786440 | tf_op jit(solution)/shard_map/ppermute | solution.py:388
  113.0 8.8 %collective-permute-start.14 = (f32[16,4096]{1,0:T(8,128)S(1)}, f32[16,4096]{1,0:T(8,128)S(1)}, u32[]{:S(2)}, u32[]{:S(2)}) collective-permute-start(f32[16,4096]{1,0:T(8,128)S(1)} %get-tuple-element.19), channel_id=1, source_target_pairs={{0,32},{32,64},{64,96},{96,0},{1,33},{33,65},{65,97},{97,1},{2,34}... | collective-permute-start | bytes 786440 | tf_op jit(solution)/shard_map/ppermute | solution.py:388
  113.6 13.4 %collective-permute-start.17 = (f32[16,4096]{1,0:T(8,128)S(1)}, f32[16,4096]{1,0:T(8,128)S(1)}, u32[]{:S(2)}, u32[]{:S(2)}) collective-permute-start(f32[16,4096]{1,0:T(8,128)S(1)} %get-tuple-element.21), channel_id=1, source_target_pairs={{0,32},{32,64},{64,96},{96,0},{1,33},{33,65},{65,97},{97,1},{2,34}... | collective-permute-start | bytes 786440 | tf_op jit(solution)/shard_map/ppermute | solution.py:388
  113.9 17.0 %collective-permute-start.16 = (f32[16,4096]{1,0:T(8,128)S(1)}, f32[16,4096]{1,0:T(8,128)S(1)}, u32[]{:S(2)}, u32[]{:S(2)}) collective-permute-start(f32[16,4096]{1,0:T(8,128)S(1)} %get-tuple-element.20), channel_id=1, source_target_pairs={{0,96},{32,0},{64,32},{96,64},{1,97},{33,1},{65,33},{97,65},{2,98}... | collective-permute-start | bytes 786440 | tf_op jit(solution)/shard_map/ppermute | solution.py:388
  119.7 11.2 %collective-permute-start.19 = (f32[16,4096]{1,0:T(8,128)S(1)}, f32[16,4096]{1,0:T(8,128)S(1)}, u32[]{:S(2)}, u32[]{:S(2)}) collective-permute-start(f32[16,4096]{1,0:T(8,128)S(1)} %add.20), channel_id=1, source_target_pairs={{0,96},{32,0},{64,32},{96,64},{1,97},{33,1},{65,33},{97,65},{2,98}... | collective-permute-start | bytes 786440 | tf_op jit(solution)/shard_map/ppermute | solution.py:388
  121.9 10.8 %collective-permute-start.15 = (f32[16,4096]{1,0:T(8,128)S(1)}, f32[16,4096]{1,0:T(8,128)S(1)}, u32[]{:S(2)}, u32[]{:S(2)}) collective-permute-start(f32[16,4096]{1,0:T(8,128)S(1)} %add.18), channel_id=1, source_target_pairs={{0,32},{32,64},{64,96},{96,0},{1,33},{33,65},{65,97},{97,1},{2,34}... | collective-permute-start | bytes 786440 | tf_op jit(solution)/shard_map/ppermute | solution.py:388

commit v2 on v1

--- a/solution.py
+++ b/solution.py
@@ -49,7 +49,7 @@
     return pl.multiple_of(x - (x & (size - 1)), size)
 
 
-def table_kernel(pos_ref, psf_ref, res_ref, out_ref, tiles, wide, acc, sems):
+def table_kernel(pos_ref, psf_ref, res_ref, out_ref, tiles, acc, packed, sems):
     row_id = place_of_rows()
     first = row_id * SLAB
     lane = lax.broadcasted_iota(jnp.int32, (SUBLANES, LANES), 1)
@@ -69,25 +69,28 @@
         tile_copy(k).start()
     sums = [jnp.zeros((SUBLANES, LANES), jnp.float32) for _ in range(STEPS // FOLD)]
     for k in range(STEPS):
-        base_row = pos_ref[0, k] + (HALF - row_id * SHARD)
-        base_col = pos_ref[1, k] + HALF
+        packed[k] = (pos_ref[0, k] << 16) + pos_ref[1, k]
+    corner = ((HALF - row_id * SHARD) << 16) + HALF
+    for k in range(STEPS):
+        base = packed[k] + corner
         for l in range(k):
-            row = base_row - pos_ref[0, l]
-            col = base_col - pos_ref[1, l]
-            foreign = (row >> 6) | (col >> 11)
-            rows = pl.ds(pl.multiple_of(row & (SHARD - SUBLANES), SUBLANES), SUBLANES)
-            cols = pl.ds(pl.multiple_of(col & (PATCH - LANES), LANES), LANES)
-            here, turned = placed(psf_ref[rows, cols], row, col, STEPS * (k % FOLD) + l, foreign)
+            place_of = base - packed[l]
+            foreign = place_of & -0x3F0800
+            rows = pl.ds(pl.multiple_of((place_of >> 16) & (SHARD - SUBLANES), SUBLANES), SUBLANES)
+            cols = pl.ds(pl.multiple_of(place_of & (PATCH - LANES), LANES), LANES)
+            target = STEPS * (k % FOLD) + l
+            turned = pltpu.roll(psf_ref[rows, cols], (target - place_of) & (LANES - 1), 1)
+            code = ((place_of >> 9) & ((SUBLANES - 1) * LANES)) + target
+            here = cell == jnp.where(foreign == 0, code, -1)
             sums[k // FOLD] = jnp.where(here, turned, sums[k // FOLD])
-        if k % FOLD == FOLD - 1:
-            wide[k // FOLD] = sums[k // FOLD]
     for k in range(STEPS):
         tile_copy(k).wait()
+    for k in range(STEPS):
         local = pos_ref[0, k] - first
         here, turned = placed(tiles[k], local, pos_ref[1, k], STEPS * (k % FOLD) + k, local >> 5)
-        wide[k // FOLD] = jnp.where(here, turned, wide[k // FOLD])
+        sums[k // FOLD] = jnp.where(here, turned, sums[k // FOLD])
     for g in range(STEPS // FOLD):
-        acc[g : g + 1, :] = jnp.sum(wide[g], axis=0, keepdims=True)
+        acc[g : g + 1, :] = jnp.sum(sums[g], axis=0, keepdims=True)
     out_ref[...] = jnp.broadcast_to(acc[...][None], (DEVICES, SUBLANES, LANES))
 
 
@@ -103,8 +106,8 @@
         out_specs=pl.BlockSpec(memory_space=pltpu.VMEM),
         scratch_shapes=[
             pltpu.VMEM((STEPS, SUBLANES, LANES), jnp.float32),
-            pltpu.VMEM((SUBLANES, SUBLANES, LANES), jnp.float32),
             pltpu.VMEM((SUBLANES, LANES), jnp.float32),
+            pltpu.SMEM((STEPS,), jnp.int32),
             pltpu.SemaphoreType.DMA((STEPS,)),
         ],
         name="table",
@@ -121,19 +124,19 @@
         for g in range(SUBLANES):
             rows[g, c : c + 1, :] = sums[0][g : g + 1, :]
             rows[g, NCHAN + c : NCHAN + c + 1, :] = jnp.zeros((1, LANES), jnp.float32)
-    lane = lax.broadcasted_iota(jnp.int32, (SUBLANES, LANES), 1)
     sub = lax.broadcasted_iota(jnp.int32, (SUBLANES, LANES), 0)
-    at = lane % STEPS
-    group = lane // STEPS
     own = sub == chan_id
-    amps = jnp.zeros((SUBLANES, LANES), jnp.float32)
-    for k in range(STEPS):
-        weights = jnp.where(at == k, -1.0, amps)
-        products = jnp.where(group == k % FOLD, rows[k // FOLD] * weights, 0.0)
-        value = -jnp.sum(products, axis=1, keepdims=True)
+    amps = []
+    for k in range(STEPS):
+        line = rows[k // FOLD]
+        at = STEPS * (k % FOLD)
+        spread = [jnp.broadcast_to(line[:, at + l : at + l + 1], (SUBLANES, LANES)) for l in range(k + 1)]
+        value = spread[k]
+        for l in range(k):
+            value = value - spread[l] * amps[l]
         total = jnp.sum(value, axis=0, keepdims=True)
-        amp = jnp.broadcast_to(0.25 * (value + total / NCHAN), (SUBLANES, LANES))
-        amps = jnp.where((at == k) & (sub < NCHAN), amp, amps)
+        amp = 0.25 * (value + total / NCHAN)
+        amps.append(jnp.where(sub < NCHAN, amp, 0.0))
         mine = jnp.sum(jnp.where(own, amp, 0.0), axis=0, keepdims=True)
         amps_ref[k] = jnp.broadcast_to(mine, (SUBLANES, LANES))
 

time: 151 us -> 147 us (0.974)
  Pallas kernels: 28.4 us -> 24.1 us
    pallas_call x1, Pallas kernels: 8.77 us -> 6.27 us  [table(): pl.pallas_call(table_kernel, out_shape=jax.ShapeDtypeStruct((DEVICES, SUB...]
    pallas_call x3, Pallas kernels: 17.8 us -> 16 us  [part(): pl.pallas_call(functools.partial(part_kernel, names, halves, late, not la...]
  transfers between devices with their start and end apart: 20 -> 20, of which waited for: 7 -> 7; matrix products, arithmetic and copies ran while one was open for 0% -> 0% of each run, Pallas kernels for 16% -> 13%
where the time goes in v2:
time: 147 us; the launch traced here: 146 us
  starting transfers between devices  47 us (32%)
  blocking collectives  35.1 us (24%)
  waiting for transfers between devices  25.1 us (17%)
  Pallas kernels  24.1 us (16%)
  local copies, waits for them, and re-layouts  10.9 us (7%)
  other arithmetic  2.52 us (2%)
  between operations  1.59 us (1%)
    ppermute x13, starting transfers between devices, permute(): return lax.ppermute(x, ROWS, pairs)  39.8 us
    all_to_all x1, blocking collectives, cycle(): parts = lax.all_to_all(parts, CHAN_ROWS, 0, 0, tiled=True)  21 us
    pallas_call x3, Pallas kernels, part(): pl.pallas_call(functools.partial(part_kernel, names, halves, late, not la...  16 us
    all_to_all x1, blocking collectives, cycle(): lax.all_to_all(square, CHAN_ROWS, 0, 0, tiled=True)[:, 0, 0]  14.2 us
    ppermute x6, waiting for transfers between devices, shift(): lax.ppermute(x, 'chan', [(i, (i + by) % NCHAN) for i in range(NCHAN)])  14 us
    ppermute x13, waiting for transfers between devices, permute(): return lax.ppermute(x, ROWS, pairs)  10.4 us
    unnamed x26, local copies, waits for them, and re-layouts  10.2 us
    ppermute x6, starting transfers between devices, shift(): lax.ppermute(x, 'chan', [(i, (i + by) % NCHAN) for i in range(NCHAN)])  6.43 us
  transfers between devices with their start and end apart: 20, of which 7 were waited for; matrix products, arithmetic and copies ran while one was open for 0% of the time, Pallas kernels for 13%

profile of v2, /device:TPU:1, one launch (start us, length us, event | category | flops | bytes accessed | tf_op | source)
XLA Modules:
  0.0 146.3 jit_solution(17108461000981420314)
XLA Ops:
  0.6 1.3 collective-permute-start.3
  1.9 0.7 collective-permute-start.4
  2.6 4.0 %collective-permute-start = (f32[64,2048]{1,0:T(8,128)}, f32[64,2048]{1,0:T(8,128)S(1)}, u32[]{:S(2)}, u32[]{:S(2)}) collective-permute-start(f32[64,2048]{1,0:T(8,128)} %bitcast.8), channel_id=1, source_target_pairs={{1,3},{2,4},{3,5},{4,6},{5,7},{6,0},{7,1},{8,10},{9,11},{10,12},{1... | collective-permute-start | bytes 1572872 | tf_op jit(solution)/shard_map/ppermute | solution.py:199
  6.7 1.3 collective-permute-start.1
  8.0 1.3 collective-permute-start.2
  9.3 6.3 %collective-permute-done.3 = f32[64,2048]{1,0:T(8,128)S(1)} collective-permute-done((f32[64,2048]{1,0:T(8,128)}, f32[64,2048]{1,0:T(8,128)S(1)}, u32[]{:S(2)}, u32[]{:S(2)}) %collective-permute-start.3) | collective-permute-done | bytes 524320 | tf_op jit(solution)/shard_map/ppermute | solution.py:199
  15.6 1.3 collective-permute-start.9
  16.9 4.1 %collective-permute-start.5 = (f32[64,2048]{1,0:T(8,128)S(1)}, f32[64,2048]{1,0:T(8,128)S(1)}, u32[]{:S(2)}, u32[]{:S(2)}) collective-permute-start(f32[64,2048]{1,0:T(8,128)S(1)} %broadcast_select_fusion.rest_4_), channel_id=1, source_target_pairs={{0,2},{1,3},{2,4},{3,5},{4,6},{5,7},{6,0},{7,1},{8,10},{9,11},{10,... | collective-permute-start | bytes 1572872 | tf_op jit(solution)/shard_map/ppermute | solution.py:199
  21.1 0.8 copy-done.4
  21.8 5.5 %collective-permute-start.6 = (f32[64,2048]{1,0:T(8,128)S(1)}, f32[64,2048]{1,0:T(8,128)S(1)}, u32[]{:S(2)}, u32[]{:S(2)}) collective-permute-start(f32[64,2048]{1,0:T(8,128)S(1)} %broadcast_select_fusion.rest_4_), channel_id=1, source_target_pairs={{0,6},{1,7},{2,0},{3,1},{4,2},{5,3},{6,4},{7,5},{8,14},{9,15},{10,... | collective-permute-start | bytes 1572872 | tf_op jit(solution)/shard_map/ppermute | solution.py:199
  27.4 0.8 copy-done.1
  28.2 4.0 %collective-permute-done.1.rest_2_ = f32[64,2048]{1,0:T(8,128)} collective-permute-done((f32[64,2048]{1,0:T(8,128)}, f32[64,2048]{1,0:T(8,128)}, u32[]{:S(2)}, u32[]{:S(2)}) %collective-permute-start.1) | collective-permute-done | bytes 524320 | tf_op jit(solution)/shard_map/ppermute | solution.py:199
  32.2 1.3 collective-permute-start.7
  33.5 0.8 copy-done.6
  34.3 1.5 %collective-permute-start.8 = (f32[64,2048]{1,0:T(8,128)}, f32[64,2048]{1,0:T(8,128)}, u32[]{:S(2)}, u32[]{:S(2)}) collective-permute-start(f32[64,2048]{1,0:T(8,128)} %collective-permute-done.1.rest_2_), channel_id=1, source_target_pairs={{16,8},{17,9},{18,10},{19,11},{20,12},{21,13},{22,14},{23,15},{8,1... | collective-permute-start | bytes 1572872 | tf_op jit(solution)/shard_map/ppermute | solution.py:199
  35.8 9.7 %collective-permute-start.11 = (f32[64,2048]{1,0:T(8,128)}, f32[64,2048]{1,0:T(8,128)}, u32[]{:S(2)}, u32[]{:S(2)}) collective-permute-start(f32[64,2048]{1,0:T(8,128)} %collective-permute-done.1.rest_2_), channel_id=1, source_target_pairs={{20,4},{21,5},{22,6},{23,7},{0,8},{1,9},{2,10},{3,11},{28,20},{29,... | collective-permute-start | bytes 1572872 | tf_op jit(solution)/shard_map/ppermute | solution.py:199
  45.4 0.8 copy-done.8
  46.2 5.9 %collective-permute-start.10 = (f32[64,2048]{1,0:T(8,128)S(1)}, f32[64,2048]{1,0:T(8,128)}, u32[]{:S(2)}, u32[]{:S(2)}) collective-permute-start(f32[64,2048]{1,0:T(8,128)S(1)} %collective-permute-done.9.rest_2_), channel_id=1, source_target_pairs={{0,2},{1,3},{2,4},{14,8},{15,9},{16,18},{17,19},{18,20},{30,24},{3... | collective-permute-start | bytes 1572872 | tf_op jit(solution)/shard_map/ppermute | solution.py:199
  52.1 0.8 copy-done.10
  52.9 2.1 %collective-permute-start.12 = (f32[64,2048]{1,0:T(8,128)S(1)}, f32[64,2048]{1,0:T(8,128)}, u32[]{:S(2)}, u32[]{:S(2)}) collective-permute-start(f32[64,2048]{1,0:T(8,128)S(1)} %collective-permute-done.9.rest_2_), channel_id=1, source_target_pairs={{0,6},{1,7},{13,11},{14,12},{15,13},{16,22},{17,23},{29,27},{30,28... | collective-permute-start | bytes 1572872 | tf_op jit(solution)/shard_map/ppermute | solution.py:199
  55.0 6.3 %table.1 = f32[128,8,128]{2,1,0:T(8,128)} custom-call(s32[2,32]{1,0:T(2,128)} %bitcast.14, f32[64,2048]{1,0:T(8,128)} %bitcast.12, f32[32,16384]{1,0:T(8,128)} %bitcast.4), custom_call_target="tpu_custom_call" | custom-call | tf_op jit(solution)/shard_map/table/pallas_call | solution.py:98
  61.3 21.0 %all_to_all.10.amps_ref = f32[128,8,128]{2,1,0:T(8,128)S(1)} all-to-all(f32[128,8,128]{2,1,0:T(8,128)} %table.1), channel_id=1, replica_groups=mesh['chan'=4,'rows_0'=4,'rows_1'=4,'rows_2'=2] {'chan','rows_0','rows_1..., dimensions={0} | all-to-all | bytes 1048576 | tf_op jit(solution)/shard_map/all_to_all | solution.py:412
  82.2 1.0 copy-done.2
  83.3 1.0 copy-done.3
  84.3 1.0 copy-done.5
  85.4 1.0 copy-done.7
  86.4 1.0 copy-done.9
  87.4 1.0 copy-done.11
  88.5 9.8 %shard_map.50 = (f32[32,8,128]{2,1,0:T(8,128)S(1)}, f32[32,16384]{1,0:T(8,128)S(1)}, f32[32,16384]{1,0:T(8,128)S(1)}) custom-call(s32[2,32]{1,0:T(2,128)S(1)} %bitcast.15, f32[128,8,128]{2,1,0:T(8,128)S(1)} %all_to_all.10.amps_ref, f32[64,2048]{1,0:T(8,128)S(1)} %bitcast.13, f32[64,2048]{1,0:T(8,128)S(1)} %copy-done.5, ...), custom_call_target="tpu_custom_call" | custom-call | tf_op jit(solution)/shard_map/pallas_call | solution.py:318
  98.3 3.1 %shard_map.52 = f32[32,16384]{1,0:T(8,128)S(1)} custom-call(s32[2,32]{1,0:T(2,128)S(1)} %bitcast.16, f32[32,8,128]{2,1,0:T(8,128)S(1)} %get-tuple-element.13.amps_ref, f32[64,2048]{1,0:T(8,128)S(1)} %collective-permute-done.7.rest_0_, f32[64,2048]{1,0:T(8,128)} %collective-permute-done.8.rest_1_, f32[64,2048]{1,0:T(8,128)S(1)} %collective-permute-done.9.rest_2_, ...), custom_call_target="tpu_custom_call" | custom-call | tf_op jit(solution)/shard_map/pallas_call | solution.py:318
  101.4 0.7 collective-permute-start.13
  102.1 3.1 %shard_map.51.mine_ref = f32[32,16384]{1,0:T(8,128)S(1)} custom-call(s32[2,32]{1,0:T(2,128)S(1)} %bitcast.17, f32[32,8,128]{2,1,0:T(8,128)S(1)} %get-tuple-element.13.amps_ref, f32[64,2048]{1,0:T(8,128)S(1)} %collective-permute-done.7.rest_0_, f32[64,2048]{1,0:T(8,128)} %collective-permute-done.8.rest_1_, f32[64,2048]{1,0:T(8,128)S(1)} %collective-permute-done.9.rest_2_, ...), custom_call_target="tpu_custom_call" | custom-call | tf_op jit(solution)/shard_map/pallas_call | solution.py:318
  105.2 0.7 collective-permute-done.13.other_ref
  105.9 1.8 %join.1 = (f32[32,16384]{1,0:T(8,128)}, f32[32,4096]{1,0:T(8,128)S(1)}, f32[16,4096]{1,0:T(8,128)S(1)}, f32[16,4096]{1,0:T(8,128)S(1)}, f32[16,4096]{1,0:T(8,128...) custom-call(f32[32,16384]{1,0:T(8,128)S(1)} %shard_map.51.mine_ref, ...), custom_call_target="tpu_custom_call" | custom-call | tf_op jit(solution)/shard_map/join/pallas_call | solution.py:368
  107.8 0.9 collective-permute-start.18
  108.7 0.6 collective-permute-start.14
  109.3 0.3 collective-permute-start.17
  109.6 2.4 %collective-permute-start.16 = (f32[16,4096]{1,0:T(8,128)S(1)}, f32[16,4096]{1,0:T(8,128)S(1)}, u32[]{:S(2)}, u32[]{:S(2)}) collective-permute-start(f32[16,4096]{1,0:T(8,128)S(1)} %get-tuple-element.20), channel_id=1, source_target_pairs={{0,96},{32,0},{64,32},{96,64},{1,97},{33,1},{65,33},{97,65},{2,98}... | collective-permute-start | bytes 786440 | tf_op jit(solution)/shard_map/ppermute | solution.py:391
  112.0 3.3 %collective-permute-done.18 = f32[16,4096]{1,0:T(8,128)S(1)} collective-permute-done((f32[16,4096]{1,0:T(8,128)S(1)}, f32[16,4096]{1,0:T(8,128)S(1)}, u32[]{:S(2)}, u32[]{:S(2)}) %collective-permute-start.18) | collective-permute-done | bytes 262176 | tf_op jit(solution)/shard_map/ppermute | solution.py:391
  115.4 2.1 %collective-permute-start.19 = (f32[16,4096]{1,0:T(8,128)S(1)}, f32[16,4096]{1,0:T(8,128)S(1)}, u32[]{:S(2)}, u32[]{:S(2)}) collective-permute-start(f32[16,4096]{1,0:T(8,128)S(1)} %add.20), channel_id=1, source_target_pairs={{0,96},{32,0},{64,32},{96,64},{1,97},{33,1},{65,33},{97,65},{2,98}... | collective-permute-start | bytes 786440 | tf_op jit(solution)/shard_map/ppermute | solution.py:391
  117.6 5.1 %collective-permute-done.17 = f32[16,4096]{1,0:T(8,128)S(1)} collective-permute-done((f32[16,4096]{1,0:T(8,128)S(1)}, f32[16,4096]{1,0:T(8,128)S(1)}, u32[]{:S(2)}, u32[]{:S(2)}) %collective-permute-start.17) | collective-permute-done | bytes 262176 | tf_op jit(solution)/shard_map/ppermute | solution.py:391
  122.7 3.8 %collective-permute-done.19 = f32[16,4096]{1,0:T(8,128)S(1)} collective-permute-done((f32[16,4096]{1,0:T(8,128)S(1)}, f32[16,4096]{1,0:T(8,128)S(1)}, u32[]{:S(2)}, u32[]{:S(2)}) %collective-permute-start.19) | collective-permute-done | bytes 262176 | tf_op jit(solution)/shard_map/ppermute | solution.py:391
  126.6 1.8 %collective-permute-done.15 = f32[16,4096]{1,0:T(8,128)S(1)} collective-permute-done((f32[16,4096]{1,0:T(8,128)S(1)}, f32[16,4096]{1,0:T(8,128)S(1)}, u32[]{:S(2)}, u32[]{:S(2)}) %collective-permute-start.15) | collective-permute-done | bytes 262176 | tf_op jit(solution)/shard_map/ppermute | solution.py:391
  128.4 0.7 multiply_reduce_fusion
  129.1 0.7 broadcast_in_dim.7
  129.8 14.2 %all_to_all.11 = f32[128,1,128]{2,1,0:T(1,128)S(1)} all-to-all(f32[128,1,128]{2,1,0:T(1,128)S(1)} %broadcast_in_dim.7), channel_id=1, replica_groups=mesh['chan'=4,'rows_0'=4,'rows_1'=4,'rows_2'=2] {'chan','rows_0','rows_1..., dimensions={0} | all-to-all | bytes 131072 | tf_op jit(solution)/shard_map/all_to_all | solution.py:425
  144.0 0.7 slice_reduce_fusion
  145.4 0.8 broadcast_multiply_fusion
  (34 shorter events, 0.3 us)
Async XLA Ops:
  0.6 15.0 %collective-permute-start.3 = (f32[64,2048]{1,0:T(8,128)}, f32[64,2048]{1,0:T(8,128)S(1)}, u32[]{:S(2)}, u32[]{:S(2)}) collective-permute-start(f32[64,2048]{1,0:T(8,128)} %bitcast.6), channel_id=1, source_target_pairs={{8,0},{9,1},{10,2},{11,3},{12,4},{13,5},{14,6},{15,7},{16,24},{17,... | collective-permute-start | bytes 1572872 | tf_op jit(solution)/shard_map/ppermute | solution.py:199
  1.9 14.9 %collective-permute-start.4 = (f32[64,2048]{1,0:T(8,128)}, f32[64,2048]{1,0:T(8,128)S(1)}, u32[]{:S(2)}, u32[]{:S(2)}) collective-permute-start(f32[64,2048]{1,0:T(8,128)} %bitcast.7), channel_id=1, source_target_pairs={{16,8},{17,9},{18,10},{19,11},{20,12},{21,13},{22,14},{23,15},{8,1... | collective-permute-start | bytes 1572872 | tf_op jit(solution)/shard_map/ppermute | solution.py:199
  2.6 18.4 %collective-permute-start = (f32[64,2048]{1,0:T(8,128)}, f32[64,2048]{1,0:T(8,128)S(1)}, u32[]{:S(2)}, u32[]{:S(2)}) collective-permute-start(f32[64,2048]{1,0:T(8,128)} %bitcast.8), channel_id=1, source_target_pairs={{1,3},{2,4},{3,5},{4,6},{5,7},{6,0},{7,1},{8,10},{9,11},{10,12},{1... | collective-permute-start | bytes 1572872 | tf_op jit(solution)/shard_map/ppermute | solution.py:199
  6.7 25.5 %collective-permute-start.1 = (f32[64,2048]{1,0:T(8,128)}, f32[64,2048]{1,0:T(8,128)}, u32[]{:S(2)}, u32[]{:S(2)}) collective-permute-start(f32[64,2048]{1,0:T(8,128)} %bitcast.9), channel_id=1, source_target_pairs={{3,7},{4,0},{5,1},{6,2},{7,3},{8,12},{9,13},{10,14},{11,15},{12,8}... | collective-permute-start | bytes 1572872 | tf_op jit(solution)/shard_map/ppermute | solution.py:199
  8.0 25.5 %collective-permute-start.2 = (f32[64,2048]{1,0:T(8,128)}, f32[64,2048]{1,0:T(8,128)S(1)}, u32[]{:S(2)}, u32[]{:S(2)}) collective-permute-start(f32[64,2048]{1,0:T(8,128)} %bitcast.10), channel_id=1, source_target_pairs={{2,0},{3,1},{4,2},{5,3},{6,4},{7,5},{8,14},{9,15},{10,8},{11,9},{1... | collective-permute-start | bytes 1572872 | tf_op jit(solution)/shard_map/ppermute | solution.py:199
  15.6 20.2 %collective-permute-start.9 = (f32[64,2048]{1,0:T(8,128)}, f32[64,2048]{1,0:T(8,128)S(1)}, u32[]{:S(2)}, u32[]{:S(2)}) collective-permute-start(f32[64,2048]{1,0:T(8,128)} %bitcast.11), channel_id=1, source_target_pairs={{16,0},{17,1},{18,2},{19,3},{4,12},{5,13},{6,14},{7,15},{24,16},{2... | collective-permute-start | bytes 1572872 | tf_op jit(solution)/shard_map/ppermute | solution.py:199
  16.9 28.5 %collective-permute-start.5 = (f32[64,2048]{1,0:T(8,128)S(1)}, f32[64,2048]{1,0:T(8,128)S(1)}, u32[]{:S(2)}, u32[]{:S(2)}) collective-permute-start(f32[64,2048]{1,0:T(8,128)S(1)} %broadcast_select_fusion.rest_4_), channel_id=1, source_target_pairs={{0,2},{1,3},{2,4},{3,5},{4,6},{5,7},{6,0},{7,1},{8,10},{9,11},{10,... | collective-permute-start | bytes 1572872 | tf_op jit(solution)/shard_map/ppermute | solution.py:199
  21.1 0.8 copy-start.4
  21.8 30.2 %collective-permute-start.6 = (f32[64,2048]{1,0:T(8,128)S(1)}, f32[64,2048]{1,0:T(8,128)S(1)}, u32[]{:S(2)}, u32[]{:S(2)}) collective-permute-start(f32[64,2048]{1,0:T(8,128)S(1)} %broadcast_select_fusion.rest_4_), channel_id=1, source_target_pairs={{0,6},{1,7},{2,0},{3,1},{4,2},{5,3},{6,4},{7,5},{8,14},{9,15},{10,... | collective-permute-start | bytes 1572872 | tf_op jit(solution)/shard_map/ppermute | solution.py:199
  27.4 0.8 copy-start.1
  32.2 66.1 %collective-permute-start.7 = (f32[64,2048]{1,0:T(8,128)}, f32[64,2048]{1,0:T(8,128)S(1)}, u32[]{:S(2)}, u32[]{:S(2)}) collective-permute-start(f32[64,2048]{1,0:T(8,128)} %collective-permute-done.1.rest_2_), channel_id=1, source_target_pairs={{8,0},{9,1},{10,2},{11,3},{12,4},{13,5},{14,6},{15,7},{16,24},{17,... | collective-permute-start | bytes 1572872 | tf_op jit(solution)/shard_map/ppermute | solution.py:199
  33.5 0.8 copy-start.6
  34.3 64.0 %collective-permute-start.8 = (f32[64,2048]{1,0:T(8,128)}, f32[64,2048]{1,0:T(8,128)}, u32[]{:S(2)}, u32[]{:S(2)}) collective-permute-start(f32[64,2048]{1,0:T(8,128)} %collective-permute-done.1.rest_2_), channel_id=1, source_target_pairs={{16,8},{17,9},{18,10},{19,11},{20,12},{21,13},{22,14},{23,15},{8,1... | collective-permute-start | bytes 1572872 | tf_op jit(solution)/shard_map/ppermute | solution.py:199
  35.8 62.6 %collective-permute-start.11 = (f32[64,2048]{1,0:T(8,128)}, f32[64,2048]{1,0:T(8,128)}, u32[]{:S(2)}, u32[]{:S(2)}) collective-permute-start(f32[64,2048]{1,0:T(8,128)} %collective-permute-done.1.rest_2_), channel_id=1, source_target_pairs={{20,4},{21,5},{22,6},{23,7},{0,8},{1,9},{2,10},{3,11},{28,20},{29,... | collective-permute-start | bytes 1572872 | tf_op jit(solution)/shard_map/ppermute | solution.py:199
  45.4 0.8 copy-start.8
  46.2 52.1 %collective-permute-start.10 = (f32[64,2048]{1,0:T(8,128)S(1)}, f32[64,2048]{1,0:T(8,128)}, u32[]{:S(2)}, u32[]{:S(2)}) collective-permute-start(f32[64,2048]{1,0:T(8,128)S(1)} %collective-permute-done.9.rest_2_), channel_id=1, source_target_pairs={{0,2},{1,3},{2,4},{14,8},{15,9},{16,18},{17,19},{18,20},{30,24},{3... | collective-permute-start | bytes 1572872 | tf_op jit(solution)/shard_map/ppermute | solution.py:199
  52.1 0.8 copy-start.10
  52.9 45.5 %collective-permute-start.12 = (f32[64,2048]{1,0:T(8,128)S(1)}, f32[64,2048]{1,0:T(8,128)}, u32[]{:S(2)}, u32[]{:S(2)}) collective-permute-start(f32[64,2048]{1,0:T(8,128)S(1)} %collective-permute-done.9.rest_2_), channel_id=1, source_target_pairs={{0,6},{1,7},{13,11},{14,12},{15,13},{16,22},{17,23},{29,27},{30,28... | collective-permute-start | bytes 1572872 | tf_op jit(solution)/shard_map/ppermute | solution.py:199
  55.0 27.3 %copy-start = (f32[1,32,16384]{2,1,0:T(8,128)S(1)}, f32[1,32,16384]{2,1,0:T(8,128)}, u32[]{:S(2)}) copy-start(f32[1,32,16384]{2,1,0:T(8,128)} %param.3) | copy-start | bytes 6291460
  55.0 27.3 %copy-start.12 = (s32[32,2]{0,1:T(2,128)S(1)}, s32[32,2]{0,1:T(2,128)}, u32[]{:S(2)}) copy-start(s32[32,2]{0,1:T(2,128)} %param.5) | copy-start | bytes 772
  82.2 1.0 copy-start.2
  83.3 1.0 copy-start.3
  84.3 1.0 copy-start.5
  85.4 1.0 copy-start.7
  86.4 1.0 copy-start.9
  87.4 1.0 copy-start.11
  101.4 4.5 %collective-permute-start.13 = (f32[32,16384]{1,0:T(8,128)S(1)}, f32[32,16384]{1,0:T(8,128)S(1)}, u32[]{:S(2)}, u32[]{:S(2)}) collective-permute-start(f32[32,16384]{1,0:T(8,128)S(1)} %shard_map.52), channel_id=1, source_target_pairs={{0,1},{1,0},{2,3},{3,2},{4,5},{5,4},{6,7},{7,6},{8,9},{9,8},{10,11... | collective-permute-start | bytes 6291464 | tf_op jit(solution)/shard_map/ppermute | solution.py:420
  107.8 7.6 %collective-permute-start.18 = (f32[16,4096]{1,0:T(8,128)S(1)}, f32[16,4096]{1,0:T(8,128)S(1)}, u32[]{:S(2)}, u32[]{:S(2)}) collective-permute-start(f32[16,4096]{1,0:T(8,128)S(1)} %get-tuple-element.23), channel_id=1, source_target_pairs={{0,96},{32,0},{64,32},{96,64},{1,97},{33,1},{65,33},{97,65},{2,98}... | collective-permute-start | bytes 786440 | tf_op jit(solution)/shard_map/ppermute | solution.py:391
  108.7 8.8 %collective-permute-start.14 = (f32[16,4096]{1,0:T(8,128)S(1)}, f32[16,4096]{1,0:T(8,128)S(1)}, u32[]{:S(2)}, u32[]{:S(2)}) collective-permute-start(f32[16,4096]{1,0:T(8,128)S(1)} %get-tuple-element.19), channel_id=1, source_target_pairs={{0,32},{32,64},{64,96},{96,0},{1,33},{33,65},{65,97},{97,1},{2,34}... | collective-permute-start | bytes 786440 | tf_op jit(solution)/shard_map/ppermute | solution.py:391
  109.3 13.4 %collective-permute-start.17 = (f32[16,4096]{1,0:T(8,128)S(1)}, f32[16,4096]{1,0:T(8,128)S(1)}, u32[]{:S(2)}, u32[]{:S(2)}) collective-permute-start(f32[16,4096]{1,0:T(8,128)S(1)} %get-tuple-element.21), channel_id=1, source_target_pairs={{0,32},{32,64},{64,96},{96,0},{1,33},{33,65},{65,97},{97,1},{2,34}... | collective-permute-start | bytes 786440 | tf_op jit(solution)/shard_map/ppermute | solution.py:391
  109.6 17.0 %collective-permute-start.16 = (f32[16,4096]{1,0:T(8,128)S(1)}, f32[16,4096]{1,0:T(8,128)S(1)}, u32[]{:S(2)}, u32[]{:S(2)}) collective-permute-start(f32[16,4096]{1,0:T(8,128)S(1)} %get-tuple-element.20), channel_id=1, source_target_pairs={{0,96},{32,0},{64,32},{96,64},{1,97},{33,1},{65,33},{97,65},{2,98}... | collective-permute-start | bytes 786440 | tf_op jit(solution)/shard_map/ppermute | solution.py:391
  115.4 11.2 %collective-permute-start.19 = (f32[16,4096]{1,0:T(8,128)S(1)}, f32[16,4096]{1,0:T(8,128)S(1)}, u32[]{:S(2)}, u32[]{:S(2)}) collective-permute-start(f32[16,4096]{1,0:T(8,128)S(1)} %add.20), channel_id=1, source_target_pairs={{0,96},{32,0},{64,32},{96,64},{1,97},{33,1},{65,33},{97,65},{2,98}... | collective-permute-start | bytes 786440 | tf_op jit(solution)/shard_map/ppermute | solution.py:391
  117.6 10.8 %collective-permute-start.15 = (f32[16,4096]{1,0:T(8,128)S(1)}, f32[16,4096]{1,0:T(8,128)S(1)}, u32[]{:S(2)}, u32[]{:S(2)}) collective-permute-start(f32[16,4096]{1,0:T(8,128)S(1)} %add.18), channel_id=1, source_target_pairs={{0,32},{32,64},{64,96},{96,0},{1,33},{33,65},{65,97},{97,1},{2,34}... | collective-permute-start | bytes 786440 | tf_op jit(solution)/shard_map/ppermute | solution.py:391
